TPU v7x, 128 devices: a whole 4x4x4 slice. The times are simulated.
128 devices in a mesh: blk: 32 (over x, y_hi, z), shard: 4 (over y_lo, core).
Axes of the slice: x: 4, y: 4 (y_hi: 2, y_lo: 2; y = y_hi * 2 + y_lo), z: 4, core: 2. Of those that a mesh axis runs over, the one named last changes fastest.
Arguments:
- tokens: bfloat16 [32768, 2048], P(('blk', 'shard')), may hold values from -6 to 6
- targets: bfloat16 [32768, 2048], P(('blk', 'shard')), may hold values from -6 to 6
- up_weight: bfloat16 [2048, 7168], P(None, 'shard'), may hold values from -0.125 to 0.125
- down_weight: bfloat16 [32, 7168, 2048], P('blk', 'shard'), may hold values from -6 to 6
- mix_numer: int32 [2, 32, 3], replicated, may hold values from 1 to 2, as said below
Outputs:
- drift: bfloat16 [32, 7168, 2048], P('blk', 'shard')
Inputs may be any that keep to these rules, and one draw needn't show every extreme that they name: Each row of mix_numer is (2, 1, 1), (1, 2, 1) or (1, 1, 2).
All inputs are finite; a program needn't handle non-finite values.
Results may differ from a plain program's by a relative error of at most 0.017.
Values may be sent and summed in bfloat16 or wider, within the bound.
A program may use at most 128 MiB of HBM per device.

v0:
```python
import jax
import jax.numpy as jnp
from jax import lax
from jax.sharding import PartitionSpec as P

FF = 7168
ROUNDS = 2


learn_rate = 2.0


def passed_along(x, axis, by):
    devices = lax.axis_size(axis)
    return lax.ppermute(x, axis, [(i, (i + by) % devices) for i in range(devices)])


def padded_to(lines, devices):
    spare = -len(lines) % devices
    return jnp.pad(lines, [(0, spare)] + [(0, 0)] * (lines.ndim - 1))


def total_of(x, axis):
    lines = x.reshape(-1, *x.shape[1:][-1:])
    padded = padded_to(lines, lax.axis_size(axis))
    own = lax.psum_scatter(padded, axis, scatter_dimension=0, tiled=True)
    whole = lax.all_gather(own, axis, axis=0, tiled=True)
    return whole[: len(lines)].reshape(x.shape)


def combine(center, left, right, weights):
    total = (
        weights[0] * center.astype(jnp.float32)
        + weights[1] * left.astype(jnp.float32)
        + weights[2] * right.astype(jnp.float32)
    )
    return (total / 4.0).astype(jnp.bfloat16)


def numer_of(mix_numer, round_index, worker):
    return lax.dynamic_index_in_dim(mix_numer[round_index], worker, 0, keepdims=False).astype(
        jnp.float32
    )


def body(tokens, targets, up_weight, down_weight, mix_numer):
    weight = down_weight[0]
    out_scale = 1.0 / jnp.sqrt(jnp.float32(FF))
    hidden = jax.nn.silu(
        jnp.dot(
            lax.all_gather(tokens, "shard", axis=0, tiled=True),
            up_weight,
            preferred_element_type=jnp.float32,
        )
    ).astype(jnp.bfloat16)
    rows = hidden
    output = lax.psum_scatter(
        (jnp.dot(rows, weight, preferred_element_type=jnp.float32) * out_scale).astype(
            jnp.bfloat16
        ),
        "shard",
        scatter_dimension=0,
        tiled=True,
    ).astype(jnp.float32)
    resid = (output - targets.astype(jnp.float32)).astype(jnp.bfloat16)
    rows = hidden
    grad = lax.dot_general(
        rows,
        lax.all_gather(resid, "shard", axis=0, tiled=True),
        (((0,), (0,)), ((), ())),
        preferred_element_type=jnp.float32,
    )
    stepped = (weight.astype(jnp.float32) - learn_rate * grad * out_scale).astype(jnp.bfloat16)
    worker = lax.axis_index("blk")
    workers = lax.axis_size("blk")
    mixed = stepped
    for round_index in range(ROUNDS):
        left = passed_along(mixed, "blk", 1)
        right = passed_along(mixed, "blk", -1)
        mixed = combine(mixed, left, right, numer_of(mix_numer, round_index, worker))
    total = total_of(mixed.astype(jnp.float32).astype(jnp.bfloat16), "blk").astype(jnp.float32)
    average = total / jnp.float32(workers)
    return (mixed.astype(jnp.float32) - average).astype(jnp.bfloat16)[None]


def solution(mesh):
    in_specs = (
        P(("blk", "shard"), None),
        P(("blk", "shard"), None),
        P(None, "shard"),
        P("blk", "shard", None),
        P(),
    )
    out_specs = P("blk", "shard", None)
    return jax.shard_map(body, mesh=mesh, in_specs=in_specs, out_specs=out_specs, check_vma=False)
```

profile of v0, /device:TPU:120, one launch (start us, length us, event | category | flops | bytes accessed | tf_op | source)
XLA Modules:
  0.0 862.2 jit_solution(7158695110332254294)
XLA Ops:
  6.5 0.7 all-gather.4.cloned.1.call-update
  7.3 47.9 %all-gather.4.cloned.1.call-done = bf16[1024,2048]{1,0:T(8,128)(2,1)} async-done(((bf16[256,2048]{1,0:T(8,128)(2,1)}), bf16[1024,2048]{1,0:T(8,128)(2,1)}) %all-gather.4.cloned.1.call-update) | async-done | bytes 4194320 | tf_op jit(solution)/shard_map/all_gather | solution.py:51
  55.2 11.7 %fusion.8 = f32[1024,1792]{1,0:T(8,128)S(1)} fusion(bf16[1024,2048]{1,0:T(8,128)(2,1)} %all-gather.4.cloned.1.call-done, bf16[2048,1792]{1,0:T(8,128)(2,1)} %param.7), kind=kOutput, calls=%fused_computation.15 | convolution fusion | flops 7516192768 | bytes 18874368 | tf_op jit(solution)/shard_map/dot_general | solution.py:50
  66.9 3.0 copy-done.2
  69.9 11.6 %multiply_convert_fusion.2 = bf16[1024,2048]{1,0:T(8,128)(2,1)} fusion(bf16[1,1792,2048]{2,1,0:T(8,128)(2,1)} %param.8, f32[1024,1792]{1,0:T(8,128)S(1)} %fusion.8), kind=kOutput, calls=%fused_computation.4 | convolution fusion | flops 7529562112 | bytes 18874368 | tf_op jit(solution)/shard_map/dot_general | solution.py:58
  81.5 0.0 all-gather.6.cloned.1.call-start
  81.6 46.9 %reduce-scatter.3.cloned.1.call-done = bf16[256,2048]{1,0:T(8,128)(2,1)} async-done(((bf16[1024,2048]{1,0:T(8,128)(2,1)}), bf16[256,2048]{1,0:T(8,128)(2,1)}) %reduce-scatter.3.cloned.1.call-update) | async-done | bytes 1048592 | tf_op jit(solution)/shard_map/reduce_scatter | solution.py:57
  128.5 2.6 subtract_convert_fusion.2
  131.2 46.9 %all-gather.6.cloned.1.call-done = bf16[1024,2048]{1,0:T(8,128)(2,1)} async-done(((bf16[256,2048]{1,0:T(8,128)(2,1)}), bf16[1024,2048]{1,0:T(8,128)(2,1)}) %all-gather.6.cloned.1.call-update) | async-done | bytes 4194320 | tf_op jit(solution)/shard_map/all_gather | solution.py:69
  178.1 15.0 %subtract_convert_fusion.1 = bf16[1792,2048]{1,0:T(8,128)(2,1)} fusion(bf16[1024,2048]{1,0:T(8,128)(2,1)} %all-gather.6.cloned.1.call-done, bf16[1,1792,2048]{2,1,0:T(8,128)(2,1)} %param.8, f32[1024,1792]{1,0:T(8,128)} %copy-done.2), kind=kOutput, calls=%fused_computation.3 | convolution fusion | flops 7540047872 | bytes 26214400 | tf_op jit(solution)/shard_map/dot_general | solution.py:67
  193.0 0.8 collective-permute-start.1
  193.8 5.8 collective-permute-start
  199.6 0.1 dynamic-slice_convert_fusion
  199.6 0.6 fusion.7
  200.2 158.4 %collective-permute-done.1 = bf16[1792,2048]{1,0:T(8,128)(2,1)} collective-permute-done((bf16[1792,2048]{1,0:T(8,128)(2,1)}, bf16[1792,2048]{1,0:T(8,128)(2,1)}, u32[]{:S(2)}, u32[]{:S(2)}) %collective-permute-start.1) | collective-permute-done | bytes 7340064 | tf_op jit(solution)/shard_map/ppermute | solution.py:15
  358.7 11.6 %multiply_convert_fusion.1 = bf16[1792,2048]{1,0:T(8,128)(2,1)S(1)} fusion(bf16[1792,2048]{1,0:T(8,128)(2,1)} %collective-permute-done.1, bf16[1792,2048]{1,0:T(8,128)(2,1)} %collective-permute-done, bf16[1792,2048]{1,0:T(8,128)(2,1)} %subtract_convert_fusion.1, f32[]{:T(128)} %bitcast.4, f32[]{:T(128)} %bitcast.3, f32[]{:T(128)} %bitcast.1), kind=kLoop, calls=%fused_computation.2 | loop fusion | flops 36700160 | bytes 29360140 | tf_op jit(solution)/shard_map/convert_element_type | solution.py:37
  370.3 0.1 collective-permute-start.3
  370.3 6.5 collective-permute-start.2
  376.9 0.6 fusion.6
  377.4 157.4 %collective-permute-done.3 = bf16[1792,2048]{1,0:T(8,128)(2,1)S(1)} collective-permute-done((bf16[1792,2048]{1,0:T(8,128)(2,1)S(1)}, bf16[1792,2048]{1,0:T(8,128)(2,1)S(1)}, u32[]{:S(2)}, u32[]{:S(2)}) %collective-permute-start.3) | collective-permute-done | bytes 7340064 | tf_op jit(solution)/shard_map/ppermute | solution.py:15
  534.8 8.2 multiply_convert_fusion
  543.1 182.2 %reduce-scatter.5.cloned.1.call-done = bf16[56,2048]{1,0:T(8,128)(2,1)} async-done(((bf16[1792,2048]{1,0:T(8,128)(2,1)}), bf16[56,2048]{1,0:T(8,128)(2,1)}) %reduce-scatter.5.cloned.1.call-update) | async-done | bytes 229392 | tf_op jit(solution)/shard_map/reduce_scatter | solution.py:26
  725.4 117.6 %all-gather.8.cloned.1.call-done = bf16[1792,2048]{1,0:T(8,128)(2,1)} async-done(((bf16[56,2048]{1,0:T(8,128)(2,1)}), bf16[1792,2048]{1,0:T(8,128)(2,1)}) %all-gather.8.cloned.1.call-update) | async-done | bytes 7340048 | tf_op jit(solution)/shard_map/all_gather | solution.py:27
  843.0 12.7 %fusion = bf16[1,1792,2048]{2,1,0:T(8,128)(2,1)} fusion(bf16[1792,2048]{1,0:T(8,128)(2,1)} %all-gather.8.cloned.1.call-done, bf16[1792,2048]{1,0:T(8,128)(2,1)} %multiply_convert_fusion), kind=kLoop, calls=%fused_computation.5 | loop fusion | flops 18350080 | bytes 22020096 | tf_op jit(solution)/shard_map/broadcast_in_dim | solution.py:83
  (16 shorter events, 0.2 us)
Async XLA Ops:
  6.5 48.7 %all-gather.4.cloned.1.call-start = ((), (), s32[]{:S(2)}) async-start(), calls=%async_computation.2 | async-start | bytes 5242880 | tf_op jit(solution)/shard_map/all_gather | solution.py:51
  7.3 121.2 %reduce-scatter.3.cloned.1.call-start = ((), (), s32[]{:S(2)}) async-start(), calls=%async_computation.3 | async-start | bytes 5242880 | tf_op jit(solution)/shard_map/reduce_scatter | solution.py:57
  66.9 3.1 copy-start.2
  69.9 58.6 %copy-start = (bf16[256,2048]{1,0:T(8,128)(2,1)S(1)}, bf16[256,2048]{1,0:T(8,128)(2,1)}, u32[]{:S(2)}) copy-start(bf16[256,2048]{1,0:T(8,128)(2,1)} %param.6) | copy-start | bytes 3145732
  81.5 96.5 %all-gather.6.cloned.1.call-start = ((), (), s32[]{:S(2)}) async-start(), calls=%async_computation.4 | async-start | bytes 5242880 | tf_op jit(solution)/shard_map/all_gather | solution.py:69
  131.1 68.4 %copy-start.1 = (s32[2,32,3]{1,0,2:T(2,128)S(1)}, s32[2,32,3]{1,0,2:T(2,128)}, u32[]{:S(2)}) copy-start(s32[2,32,3]{1,0,2:T(2,128)} %param.9) | copy-start | bytes 2308
  131.1 594.2 %reduce-scatter.5.cloned.1.call-start = ((), (), s32[]{:S(2)}) async-start(), calls=%async_computation.5 | async-start | bytes 7569408 | tf_op jit(solution)/shard_map/reduce_scatter | solution.py:26
  193.0 165.7 %collective-permute-start.1 = (bf16[1792,2048]{1,0:T(8,128)(2,1)}, bf16[1792,2048]{1,0:T(8,128)(2,1)}, u32[]{:S(2)}, u32[]{:S(2)}) collective-permute-start(bf16[1792,2048]{1,0:T(8,128)(2,1)} %subtract_convert_fusion.1), channel_id=1, source_target_pairs={{0,124},{4,0},{8,4},{12,8},{16,12},{20,16},{24,20},{28,24},{32,28}... | collective-permute-start | bytes 22020104 | tf_op jit(solution)/shard_map/ppermute | solution.py:15
  193.8 164.9 %collective-permute-start = (bf16[1792,2048]{1,0:T(8,128)(2,1)}, bf16[1792,2048]{1,0:T(8,128)(2,1)}, u32[]{:S(2)}, u32[]{:S(2)}) collective-permute-start(bf16[1792,2048]{1,0:T(8,128)(2,1)} %subtract_convert_fusion.1), channel_id=1, source_target_pairs={{0,4},{4,8},{8,12},{12,16},{16,20},{20,24},{24,28},{28,32},{32,36}... | collective-permute-start | bytes 22020104 | tf_op jit(solution)/shard_map/ppermute | solution.py:15
  370.3 164.6 %collective-permute-start.3 = (bf16[1792,2048]{1,0:T(8,128)(2,1)S(1)}, bf16[1792,2048]{1,0:T(8,128)(2,1)S(1)}, u32[]{:S(2)}, u32[]{:S(2)}) collective-permute-start(bf16[1792,2048]{1,0:T(8,128)(2,1)S(1)} %multiply_convert_fusion.1), channel_id=1, source_target_pairs={{0,124},{4,0},{8,4},{12,8},{16,12},{20,16},{24,20},{28,24},{32,28}... | collective-permute-start | bytes 22020104 | tf_op jit(solution)/shard_map/ppermute | solution.py:15
  370.3 164.5 %collective-permute-start.2 = (bf16[1792,2048]{1,0:T(8,128)(2,1)S(1)}, bf16[1792,2048]{1,0:T(8,128)(2,1)S(1)}, u32[]{:S(2)}, u32[]{:S(2)}) collective-permute-start(bf16[1792,2048]{1,0:T(8,128)(2,1)S(1)} %multiply_convert_fusion.1), channel_id=1, source_target_pairs={{0,4},{4,8},{8,12},{12,16},{16,20},{20,24},{24,28},{28,32},{32,36}... | collective-permute-start | bytes 22020104 | tf_op jit(solution)/shard_map/ppermute | solution.py:15
  543.1 299.9 %all-gather.8.cloned.1.call-start = ((), (), s32[]{:S(2)}) async-start(), calls=%async_computation.6 | async-start | bytes 7569408 | tf_op jit(solution)/shard_map/all_gather | solution.py:27
Sparse Core Ops, SparseCore 0:
  9.0 46.1 all-gather.3
  81.6 46.7 reduce-scatter.2
  131.2 46.7 all-gather.5
  543.2 182.1 reduce-scatter.4
  728.3 114.6 all-gather.7
where the time goes:
time: 866 us; the launch traced here: 862 us
  waiting for transfers between devices  758 us (88%)
  matrix products  38.2 us (4%)
  other arithmetic  35.2 us (4%)
  starting transfers between devices  13.3 us (2%)
  between operations  13.2 us (2%)
    ppermute x4, waiting for transfers between devices, passed_along(): lax.ppermute(x, axis, [(i, (i + by) % devices) for i in range(devices)])  316 us
    reduce_scatter x1, waiting for transfers between devices, total_of(): own = lax.psum_scatter(padded, axis, scatter_dimension=0, tiled=True)  182 us
    all_gather x1, waiting for transfers between devices, total_of(): whole = lax.all_gather(own, axis, axis=0, tiled=True)  118 us
    all_gather x1, waiting for transfers between devices, body(): lax.all_gather(tokens, 'shard', axis=0, tiled=True)  47.9 us
    reduce_scatter x1, waiting for transfers between devices, body(): lax.psum_scatter((jnp.dot(rows, weight, preferred_element_type=jnp.float3...  46.9 us
    all_gather x1, waiting for transfers between devices, body(): lax.all_gather(resid, 'shard', axis=0, tiled=True)  46.9 us
    convert_element_type x2, other arithmetic, combine(): return (total / 4.0).astype(jnp.bfloat16)  19.8 us
  transfers between devices with their start and end apart: 9, of which 7 were waited for; matrix products, arithmetic and copies ran while one was open for 0% of the time, Pallas kernels for 0%

commit v1 on v0

v1 whole, which is shorter than its diff:
```python
import functools
import jax
import jax.numpy as jnp
from jax import lax
from jax.experimental import pallas as pl
from jax.experimental.pallas import tpu as pltpu
from jax.sharding import PartitionSpec as P

MESH = pl.DeviceIdType.MESH
LEARN_RATE = 2.0
NW = 32
CH = 16
DEPTH = 2
F32 = jnp.float32
BF16 = jnp.bfloat16


def place():
    b, s = lax.axis_index("blk"), lax.axis_index("shard")
    return b, s, b // 8, (b // 4) % 2, b % 4


def gossip(numer, s, out, l1, r1, l2, r2, avg, rsx, piece, yrx, zrx,
           gs, gr, xs, xr, ys, yr, zs, zr, os):
    b, sh, x, yh, z = place()
    rows, width = s.shape[1], s.shape[2]
    chunks = s.shape[0]
    groups = 4
    per = chunks // groups
    quarter, half = rows // 4, rows // 8
    left, right = ((b + 31) % 32, sh), ((b + 1) % 32, sh)

    def at(xx, yy, zz):
        return (xx * 8 + yy * 4 + zz, sh)

    inner = jnp.logical_or(z == 1, z == 2)
    outer = jnp.logical_or(z == 0, z == 3)
    ydev = at(x, 1 - yh, z)
    zdev = at(x, yh, 3 - z)
    back = jnp.logical_and(yh == 1, z == 3)
    step = jnp.where(back, 3, 1)
    xnext = at((x + step) % 4, yh, z)

    barrier = pltpu.get_barrier_semaphore()
    for dev in (left, right, at((x + 1) % 4, yh, z), at((x + 2) % 4, yh, z), at((x + 3) % 4, yh, z),
                ydev, at(x, yh, (z + 1) % 4), at(x, yh, (z + 3) % 4)):
        pl.semaphore_signal(barrier, inc=1, device_id=dev, device_id_type=MESH)
    pl.semaphore_wait(barrier, 8)

    def n(r, k, j):
        return numer[r * 96 + k * 3 + j].astype(F32)

    kl, kr, kll, krr = (b + 31) % 32, (b + 1) % 32, (b + 30) % 32, (b + 2) % 32

    def v(k0, k, k1):
        return n(1, k, 0) + n(1, k1, 1) + n(1, k0, 2)

    vb, vl, vr = v(kl, b, kr), v(kll, kl, b), v(b, kr, krr)
    vll, vrr = v((b + 29) % 32, kll, kl), v(kr, krr, (b + 3) % 32)
    wb = (n(0, b, 0) * vb + n(0, kr, 1) * vr + n(0, kl, 2) * vl) * (1.0 / 16)
    wl = (n(0, kl, 0) * vl + n(0, b, 1) * vb + n(0, kll, 2) * vll) * (1.0 / 16)
    wr = (n(0, kr, 0) * vr + n(0, krr, 1) * vrr + n(0, b, 2) * vb) * (1.0 / 16)
    wl = jnp.where(z == 1, wl, 0.0)
    wr = jnp.where(z == 2, wr, 0.0)
    m = [[n(r, b, j) * 0.25 for j in range(3)] for r in range(2)]

    def send(src, dst, ss, rs, dev):
        return pltpu.make_async_remote_copy(src, dst, ss, rs, device_id=dev, device_id_type=MESH)

    def items(i):
        c = i % chunks
        src, dl, dr = (s, l1, r1) if i < chunks else (l1, l2, r2)
        return (send(src.at[c], dl.at[c], gs.at[0, i], gr.at[0, i], right),
                send(src.at[c], dr.at[c], gs.at[1, i], gr.at[1, i], left))

    BR = 128

    def over(total, body):
        def one(i, _):
            body(pl.ds(pl.multiple_of(i * BR, BR), BR))
            return 0
        lax.fori_loop(0, total // BR, one, 0)

    def first(c):
        def body(d):
            a = s[c, d, :].astype(F32)
            p = l1[c, d, :].astype(F32)
            q = r1[c, d, :].astype(F32)
            l1[c, d, :] = (m[0][0] * a + m[0][1] * p + m[0][2] * q).astype(BF16)
            r1[c, d, :] = (wb * a + wl * p + wr * q).astype(BF16)
        over(rows, body)

    def second(c):
        def body(d):
            a = l1[c, d, :].astype(F32)
            p = l2[c, d, :].astype(F32)
            q = r2[c, d, :].astype(F32)
            l2[c, d, :] = (m[1][0] * a + m[1][1] * p + m[1][2] * q).astype(BF16)
        over(rows, body)

    def last(c):
        def body(d):
            l2[c, d, :] = (l2[c, d, :].astype(F32) - avg[c, d, :].astype(F32)).astype(BF16)
        over(rows, body)
        pltpu.make_async_copy(l2.at[c], out.at[:, pl.ds(c * width, width)], os.at[c]).start()

    def own(g, xx, lo, size):
        return (pl.ds(g * per, per), pl.ds(pl.multiple_of(xx * quarter + lo, 32), size), slice(None))

    def a_rs(g, j):
        xx = (x + j) % 4
        return send(r1.at[own(g, xx, 0, quarter)], rsx.at[j - 1, pl.ds(g * per, per)],
                    xs.at[0, g, j - 1], xr.at[0, g, j - 1], at(xx, yh, z))

    def a_y(g):
        return send(piece.at[pl.ds(g * per, per), pl.ds(pl.multiple_of((1 - yh) * half, 32), half)],
                    yrx.at[pl.ds(g * per, per)], ys.at[0, g], yr.at[0, g], ydev)

    def a_z(g):
        return send(piece.at[pl.ds(g * per, per), pl.ds(pl.multiple_of(yh * half, 32), half)],
                    zrx.at[pl.ds(g * per, per)], zs.at[0, g], zr.at[0, g], zdev)

    def a_yg(g):
        ref = avg.at[own(g, x, yh * half, half)]
        return send(ref, ref, ys.at[1, g], yr.at[1, g], ydev)

    def a_zb(g):
        ref = avg.at[own(g, x, 0, quarter)]
        return send(ref, ref, zs.at[1, g], zr.at[1, g], at(x, yh, jnp.where(z == 1, 0, 3)))

    def a_x(g, k):
        ref = avg.at[own(g, (x - k * step + 16) % 4, 0, quarter)]
        return send(ref, ref, xs.at[1, g, k], xr.at[1, g, k], xnext)

    def when(cond, f):
        pl.when(cond)(f)

    def e_rs(g):
        def go():
            for j in (1, 2, 3):
                a_rs(g, j).start()
        when(inner, go)

    def e_y(g):
        def go():
            for j in (1, 2, 3):
                a_rs(g, j).wait_recv()
            for cc in range(per):
                c = g * per + cc
                def one(i, _):
                    d = pl.ds(pl.multiple_of(i * 64, 64), 64)
                    o = pl.ds(pl.multiple_of(x * quarter + i * 64, 64), 64)
                    t = r1[c, o, :].astype(F32)
                    for j in range(3):
                        t += rsx[j, c, d, :].astype(F32)
                    piece[c, d, :] = t.astype(BF16)
                    return 0
                lax.fori_loop(0, quarter // 64, one, 0)
            a_y(g).start()
        when(inner, go)

    def add_half(g, other, scale, dst):
        for cc in range(per):
            c = g * per + cc
            def one(i, _):
                d = pl.ds(pl.multiple_of(i * 32, 32), 32)
                o = pl.ds(pl.multiple_of(yh * half + i * 32, 32), 32)
                t = piece[c, o, :].astype(F32) + other[c, d, :].astype(F32)
                if scale is None:
                    piece[c, o, :] = t.astype(BF16)
                else:
                    p = pl.ds(pl.multiple_of(x * quarter + yh * half + i * 32, 32), 32)
                    avg[c, p, :] = (t * scale).astype(BF16)
                return 0
            lax.fori_loop(0, half // 32, one, 0)

    def e_z(g):
        def go():
            a_y(g).wait_recv()
            add_half(g, yrx, None, piece)
            a_z(g).start()
        when(inner, go)

    def e_yg(g):
        def go():
            a_z(g).wait_recv()
            add_half(g, zrx, 1.0 / NW, avg)
            a_yg(g).start()
        when(inner, go)

    def e_zb(g):
        def go():
            a_yg(g).wait_recv()
            a_zb(g).start()
        when(inner, go)

    def e_x0(g):
        when(outer, lambda: a_zb(g).wait_recv())
        a_x(g, 0).start()

    def e_x(g, k):
        a_x(g, k).wait_recv()
        if k < 2:
            a_x(g, k + 1).start()

    events = {}
    for g in range(groups):
        base = per * g + per - 1
        plan = [(0, e_rs), (2, e_y), (3, e_z), (6, e_yg), (7, e_zb), (10, e_x0)]
        plan += [(11 + k, functools.partial(e_x, k=k)) for k in range(3)]
        for at_slot, f in plan:
            events.setdefault(base + at_slot, []).append(functools.partial(f, g))

    for i in range(DEPTH):
        for cp in items(i):
            cp.start()
    ready = []
    for slot in range(2 * chunks):
        for cp in items(slot):
            cp.wait_recv()
        if slot < chunks:
            first(slot)
        else:
            second(slot - chunks)
        if slot + DEPTH < 2 * chunks:
            for cp in items(slot + DEPTH):
                cp.start()
        for f in events.get(slot, ()):
            f()
        if slot >= chunks:
            ready.append(slot - chunks)
            done = [c for c in ready if per * (c // per) + per - 1 + 13 <= slot]
            for c in done:
                last(c)
                ready.remove(c)
    assert not ready
    for i in range(2 * chunks):
        for cp in items(i):
            cp.wait_send()
    for g in range(groups):
        def drain():
            for j in (1, 2, 3):
                a_rs(g, j).wait_send()
            for f in (a_y, a_z, a_yg, a_zb):
                f(g).wait_send()
        when(inner, drain)
        for k in range(3):
            a_x(g, k).wait_send()
    for c in range(chunks):
        pltpu.make_async_copy(l2.at[c], out.at[:, pl.ds(c * width, width)], os.at[c]).wait()


def gossip_call(numer, s):
    chunks, rows, width = s.shape
    big = pltpu.VMEM(s.shape, BF16)
    q, h = rows // 4, rows // 8
    D = pltpu.SemaphoreType.DMA
    return pl.pallas_call(
        gossip,
        out_shape=jax.ShapeDtypeStruct((rows, chunks * width), BF16),
        in_specs=[pl.BlockSpec(memory_space=pltpu.SMEM), pl.BlockSpec(memory_space=pltpu.VMEM)],
        out_specs=pl.BlockSpec(memory_space=pl.ANY),
        scratch_shapes=[big] * 5 + [
            pltpu.VMEM((3, chunks, q, width), BF16),
            pltpu.VMEM((chunks, q, width), BF16),
            pltpu.VMEM((chunks, h, width), BF16),
            pltpu.VMEM((chunks, h, width), BF16),
            D((2, 2 * chunks)), D((2, 2 * chunks)), D((2, 4, 3)), D((2, 4, 3)),
            D((2, 4)), D((2, 4)), D((2, 4)), D((2, 4)), D((chunks,)),
        ],
        compiler_params=pltpu.CompilerParams(collective_id=0, has_side_effects=True, vmem_limit_bytes=62 * 2**20),
        name="gossip",
    )(numer, s)


def body(tokens, targets, up_weight, down_weight, mix_numer):
    weight = down_weight[0]
    ff = weight.shape[0] * lax.axis_size("shard")
    out_scale = 1.0 / jnp.sqrt(F32(ff))
    hidden = jax.nn.silu(
        jnp.dot(lax.all_gather(tokens, "shard", axis=0, tiled=True), up_weight, preferred_element_type=F32)
    ).astype(BF16)
    output = lax.psum_scatter(
        (jnp.dot(hidden, weight, preferred_element_type=F32) * out_scale).astype(BF16),
        "shard", scatter_dimension=0, tiled=True,
    ).astype(F32)
    resid = (output - targets.astype(F32)).astype(BF16)
    grad = lax.dot_general(
        hidden, lax.all_gather(resid, "shard", axis=0, tiled=True),
        (((0,), (0,)), ((), ())), preferred_element_type=F32,
    )
    stepped = (weight.astype(F32) - LEARN_RATE * grad * out_scale).astype(BF16)
    rows, cols = stepped.shape
    chunked = stepped.reshape(rows, CH, cols // CH).transpose(1, 0, 2)
    return gossip_call(mix_numer.reshape(-1), chunked)[None]


def solution(mesh):
    in_specs = (P(("blk", "shard"), None), P(("blk", "shard"), None), P(None, "shard"), P("blk", "shard", None), P())
    return jax.shard_map(body, mesh=mesh, in_specs=in_specs, out_specs=P("blk", "shard", None), check_vma=False)
```

time: 866 us -> 597 us (0.69)
  waiting for transfers between devices: 758 us -> 141 us
  Pallas kernels: 0 us -> 366 us
  other arithmetic: 35.2 us -> 2.58 us
  local copies, waits for them, and re-layouts: 4.2 us -> 31.3 us
  starting transfers between devices: 13.3 us -> 0.26 us
    pallas_call x0 -> x1, Pallas kernels: none -> 366 us  [gossip_call(): pl.pallas_call(gossip, out_shape=jax.ShapeDtypeStruct((rows, chunks * wid...]
    ppermute x4 -> x0, waiting for transfers between devices: 316 us -> none  [passed_along(): lax.ppermute(x, axis, [(i, (i + by) % devices) for i in range(devices)])]
    reduce_scatter x2 -> x1, waiting for transfers between devices: 229 us -> 46.7 us  [body(): lax.psum_scatter((jnp.dot(hidden, weight, preferred_element_type=F32) * o...]
    all_gather x1 -> x0, waiting for transfers between devices: 118 us -> none  [total_of(): whole = lax.all_gather(own, axis, axis=0, tiled=True)]
    convert_element_type x4 -> x1, other arithmetic: 22.5 us -> 2.58 us  [body(): resid = (output - targets.astype(F32)).astype(BF16)]
    ppermute x4 -> x0, starting transfers between devices: 13.1 us -> none  [passed_along(): lax.ppermute(x, axis, [(i, (i + by) % devices) for i in range(devices)])]
    broadcast_in_dim x1 -> x0, other arithmetic: 12.7 us -> none  [body(): return (mixed.astype(jnp.float32) - average).astype(jnp.bfloat16)[None]]
    reshape x0 -> x2, local copies, waits for them, and re-layouts: none -> 10.7 us  [the longest x1 10 us: body(): chunked = stepped.reshape(rows, CH, cols // CH).transpose(1, 0, 2)]
  transfers between devices with their start and end apart: 9 -> 3, of which waited for: 7 -> 3; matrix products, arithmetic and copies ran while one was open for 0% -> 0% of each run, Pallas kernels for 0% -> 0%
where the time goes in v1:
time: 597 us; the launch traced here: 593 us
  Pallas kernels  366 us (61%)
  waiting for transfers between devices  141 us (24%)
  matrix products  38.1 us (6%)
  local copies, waits for them, and re-layouts  31.3 us (5%)
  between operations  13.1 us (2%)
    pallas_call x1, Pallas kernels, gossip_call(): pl.pallas_call(gossip, out_shape=jax.ShapeDtypeStruct((rows, chunks * wid...  366 us
    all_gather x1, waiting for transfers between devices, body(): lax.all_gather(tokens, 'shard', axis=0, tiled=True)  47.9 us
    reduce_scatter x1, waiting for transfers between devices, body(): lax.psum_scatter((jnp.dot(hidden, weight, preferred_element_type=F32) * o...  46.7 us
    all_gather x1, waiting for transfers between devices, body(): lax.all_gather(resid, 'shard', axis=0, tiled=True)  46.1 us
    dot_general x1, matrix products, body(): lax.dot_general(hidden, lax.all_gather(resid, 'shard', axis=0, tiled=True...  14.9 us
  transfers between devices with their start and end apart: 3, of which 3 were waited for; matrix products, arithmetic and copies ran while one was open for 0% of the time, Pallas kernels for 0%

profile of v1, /device:TPU:120, one launch (start us, length us, event | category | flops | bytes accessed | tf_op | source)
XLA Modules:
  0.0 592.6 jit_solution(15266172510185022402)
XLA Ops:
  6.5 0.0 all-gather.3.cloned.1.call-start
  6.5 0.7 all-gather.3.cloned.1.call-update
  7.3 0.0 reduce-scatter.2.cloned.1.call-start
  7.3 47.9 %all-gather.3.cloned.1.call-done = bf16[1024,2048]{1,0:T(8,128)(2,1)} async-done(((bf16[256,2048]{1,0:T(8,128)(2,1)}), bf16[1024,2048]{1,0:T(8,128)(2,1)}) %all-gather.3.cloned.1.call-update) | async-done | bytes 4194320 | tf_op jit(solution)/shard_map/all_gather | solution.py:281
  55.2 11.7 %fusion.4 = f32[1024,1792]{1,0:T(8,128)S(1)} fusion(bf16[1024,2048]{1,0:T(8,128)(2,1)} %all-gather.3.cloned.1.call-done, bf16[2048,1792]{1,0:T(8,128)(2,1)} %param.7), kind=kOutput, calls=%fused_computation.6 | convolution fusion | flops 7516192768 | bytes 18874368 | tf_op jit(solution)/shard_map/dot_general | solution.py:281
  66.9 0.0 copy-start.2
  66.9 3.0 copy-done.2
  69.9 0.0 copy-start
  69.9 11.6 %multiply_convert_fusion = bf16[1024,2048]{1,0:T(8,128)(2,1)} fusion(bf16[1,1792,2048]{2,1,0:T(8,128)(2,1)} %param.8, f32[1024,1792]{1,0:T(8,128)S(1)} %fusion.4), kind=kOutput, calls=%fused_computation.1 | convolution fusion | flops 7529562112 | bytes 18874368 | tf_op jit(solution)/shard_map/dot_general | solution.py:284
  81.5 0.0 reduce-scatter.2.cloned.1.call-update
  81.5 0.2 all-gather.5.cloned.1.call-start
  81.7 46.7 %reduce-scatter.2.cloned.1.call-done = bf16[256,2048]{1,0:T(8,128)(2,1)} async-done(((bf16[1024,2048]{1,0:T(8,128)(2,1)}), bf16[256,2048]{1,0:T(8,128)(2,1)}) %reduce-scatter.2.cloned.1.call-update) | async-done | bytes 1048592 | tf_op jit(solution)/shard_map/reduce_scatter | solution.py:283
  128.5 0.0 copy-done
  128.5 2.6 subtract_convert_fusion.1
  131.1 0.0 all-gather.5.cloned.1.call-update
  131.1 0.0 copy-done.1
  131.1 0.1 copy.6
  131.2 0.7 reshape.6.numer
  131.9 46.1 %all-gather.5.cloned.1.call-done = bf16[1024,2048]{1,0:T(8,128)(2,1)} async-done(((bf16[256,2048]{1,0:T(8,128)(2,1)}), bf16[1024,2048]{1,0:T(8,128)(2,1)}) %all-gather.5.cloned.1.call-update) | async-done | bytes 4194320 | tf_op jit(solution)/shard_map/all_gather | solution.py:289
  178.0 14.9 %subtract_convert_fusion = bf16[1792,2048]{1,0:T(8,128)(2,1)} fusion(bf16[1024,2048]{1,0:T(8,128)(2,1)} %all-gather.5.cloned.1.call-done, bf16[1,1792,2048]{2,1,0:T(8,128)(2,1)} %param.8, f32[1024,1792]{1,0:T(8,128)} %copy-done.2), kind=kOutput, calls=%fused_computation | convolution fusion | flops 7540047872 | bytes 26214400 | tf_op jit(solution)/shard_map/dot_general | solution.py:288
  192.9 9.9 %copy.7 = bf16[1792,2048]{0,1:T(8,128)(2,1)} copy(bf16[1792,2048]{1,0:T(8,128)(2,1)} %subtract_convert_fusion) | data formatting | bytes 14680064 | tf_op jit(solution)/shard_map/convert_element_type | solution.py:292
  202.8 10.0 %copy.8 = bf16[1792,16,128]{2,0,1:T(8,128)(2,1)} copy(bf16[1792,16,128]{0,2,1:T(8,128)(2,1)} %bitcast.12) | data formatting | bytes 14680064 | tf_op jit(solution)/shard_map/reshape | solution.py:294
  212.8 365.7 %gossip.1 = bf16[1792,2048]{1,0:T(8,128)(2,1)} custom-call(s32[192]{0:T(256)} %reshape.6.numer, bf16[16,1792,128]{2,1,0:T(8,128)(2,1)} %bitcast.13), custom_call_target="tpu_custom_call" | custom-call | tf_op jit(solution)/shard_map/gossip/pallas_call | solution.py:258
  578.6 7.5 %copy.10 = bf16[1,1792,2048]{2,1,0:T(8,128)(2,1)} copy(bf16[1,1792,2048]{2,1,0:T(8,128)(2,1)} %bitcast.14) | data formatting | bytes 14680064
  (1 shorter events, 0.0 us)
Async XLA Ops:
  6.5 48.7 %all-gather.3.cloned.1.call-start = ((), (), s32[]{:S(2)}) async-start(), calls=%async_computation.1 | async-start | bytes 5242880 | tf_op jit(solution)/shard_map/all_gather | solution.py:281
  7.3 121.2 %reduce-scatter.2.cloned.1.call-start = ((), (), s32[]{:S(2)}) async-start(), calls=%async_computation.2 | async-start | bytes 5242880 | tf_op jit(solution)/shard_map/reduce_scatter | solution.py:283
  66.9 3.1 copy-start.2
  69.9 58.6 %copy-start = (bf16[256,2048]{1,0:T(8,128)(2,1)S(1)}, bf16[256,2048]{1,0:T(8,128)(2,1)}, u32[]{:S(2)}) copy-start(bf16[256,2048]{1,0:T(8,128)(2,1)} %param.6) | copy-start | bytes 3145732
  81.5 49.6 %copy-start.1 = (s32[2,32,3]{1,0,2:T(2,128)S(1)}, s32[2,32,3]{1,0,2:T(2,128)}, u32[]{:S(2)}) copy-start(s32[2,32,3]{1,0,2:T(2,128)} %param.9) | copy-start | bytes 2308
  81.5 96.5 %all-gather.5.cloned.1.call-start = ((), (), s32[]{:S(2)}) async-start(), calls=%async_computation.3 | async-start | bytes 5242880 | tf_op jit(solution)/shard_map/all_gather | solution.py:289
Sparse Core Ops, SparseCore 0:
  9.0 46.1 all-gather.2
  81.6 46.7 reduce-scatter.1
  131.2 46.7 all-gather.4

commit v2 on v1

v2 whole, which is shorter than its diff:
```python
import jax
import jax.numpy as jnp
from jax import lax
from jax.experimental import pallas as pl
from jax.experimental.pallas import tpu as pltpu
from jax.sharding import PartitionSpec as P

MESH = pl.DeviceIdType.MESH
LEARN_RATE = 2.0
NW = 32
DEPTH = 2
EARLY = 10
F32 = jnp.float32
BF16 = jnp.bfloat16


def dot(a, b):
    return jnp.dot(a, b, preferred_element_type=F32)


def kernel(numer, tokens, targets, up, weight, out,
           s, l1, r1, l2, r2, avg, rsx, piece, yrx, zrx, tok, hid, qrx, rrx, pown,
           ls, ts, tr, ps, pr, qs, qr, rs, rr,
           gs, gr, xs, xr, as_, ar, ys, yr, zs, zr, os):
    b, sh = lax.axis_index("blk"), lax.axis_index("shard")
    x, yh, z = b // 8, (b // 4) % 2, b % 4
    yl, e = sh // 2, sh % 2
    slabs, rows, width = s.shape
    chunks, cr = 2 * slabs, rows // 2
    ff, dim = 4 * rows, slabs * width
    groups, per = 4, slabs // 4
    quarter, half = rows // 4, rows // 8
    trow = tokens.shape[0]
    tp = trow // 2

    def at(xx, yy, zz):
        return (xx * 8 + yy * 4 + zz, sh)

    left, right = ((b + 31) % 32, sh), ((b + 1) % 32, sh)
    core, mate = (b, 2 * yl + 1 - e), (b, 2 * (1 - yl) + e)
    ydev = at(x, 1 - yh, z)
    zdev = at(x, yh, 3 - z)
    xp, xm = at((x + 1) % 4, yh, z), at((x + 3) % 4, yh, z)
    inner = jnp.logical_or(z == 1, z == 2)
    outer = jnp.logical_or(z == 0, z == 3)

    def send(src, dst, ss, rsem, dev):
        return pltpu.make_async_remote_copy(src, dst, ss, rsem, device_id=dev, device_id_type=MESH)

    def up_a(j):
        return pltpu.make_async_copy(up.at[pl.ds(0, rows), pl.ds(j * width, width)], l2.at[j], ls.at[0, j])

    def up_b(j):
        return pltpu.make_async_copy(up.at[pl.ds(rows, dim - rows), pl.ds(j * width, width)],
                                     l2.at[slabs - 1, pl.ds(j * width, width)], ls.at[1, j])

    def w_in(c):
        return pltpu.make_async_copy(weight.at[0, :, pl.ds(c * width, width)], s.at[c], ls.at[2, c])

    def t_in(c):
        return pltpu.make_async_copy(targets.at[:, pl.ds(c * width, width)], piece.at[c, pl.ds(0, trow)], ls.at[3, c])

    def which(p, core_at):
        return p + core_at - 2 * p * core_at

    def spot(p, chip, core_from, core_at):
        at_row = (which(p, core_at) * 2 + chip) * trow + core_from * tp
        return pl.ds(pl.multiple_of(at_row, tp), tp)

    def own_in(p):
        return pltpu.make_async_copy(tokens.at[pl.ds(p * tp, tp)], tok.at[spot(p, yl, e, e)], ls.at[4, p])

    def t_core(p):
        return send(tokens.at[pl.ds(p * tp, tp)], tok.at[spot(p, yl, e, 1 - e)], ts.at[0, p], tr.at[0, p], core)

    def t_mate(p):
        return send(tokens.at[pl.ds(p * tp, tp)], tok.at[spot(p, yl, e, e)], ts.at[1, p], tr.at[1, p], mate)

    def t_fwd(p):
        return send(tok.at[spot(p, 1 - yl, e, e)], tok.at[spot(p, 1 - yl, e, 1 - e)], ts.at[2, p], tr.at[2, p], core)

    for p in range(2):
        own_in(p).start()
    for j in range(rows // width):
        up_a(j).start()
        up_b(j).start()

    barrier = pltpu.get_barrier_semaphore()
    for dev in (core, mate, left, right, xp, at((x + 2) % 4, yh, z), xm,
                ydev, at(x, yh, (z + 1) % 4), at(x, yh, (z + 3) % 4)):
        pl.semaphore_signal(barrier, inc=1, device_id=dev, device_id_type=MESH)
    pl.semaphore_wait(barrier, 10)

    for p in range(2):
        t_mate(p).start()
    for p in range(2):
        t_core(p).start()
    for c in range(slabs):
        w_in(c).start()
        t_in(c).start()

    def n(r, k, j):
        return numer[r * 96 + k * 3 + j].astype(F32)

    kl, kr, kll, krr = (b + 31) % 32, (b + 1) % 32, (b + 30) % 32, (b + 2) % 32

    def v(k0, k, k1):
        return n(1, k, 0) + n(1, k1, 1) + n(1, k0, 2)

    vb, vl, vr = v(kl, b, kr), v(kll, kl, b), v(b, kr, krr)
    vll, vrr = v((b + 29) % 32, kll, kl), v(kr, krr, (b + 3) % 32)
    wb = (n(0, b, 0) * vb + n(0, kr, 1) * vr + n(0, kl, 2) * vl) * (1.0 / 16)
    wl = (n(0, kl, 0) * vl + n(0, b, 1) * vb + n(0, kll, 2) * vll) * (1.0 / 16)
    wr = (n(0, kr, 0) * vr + n(0, krr, 1) * vrr + n(0, b, 2) * vb) * (1.0 / 16)
    wl = jnp.where(z == 1, wl, 0.0)
    wr = jnp.where(z == 2, wr, 0.0)
    m = [[n(r, b, j) * 0.25 for j in range(3)] for r in range(2)]

    def hidden(p, chip):
        t = which(p, e) * 2 + chip
        d = pl.ds(pl.multiple_of(t * trow, trow), trow)

        def one(j, _):
            lanes = pl.ds(pl.multiple_of(j * width, width), width)
            a = dot(tok[d, :rows], l2[j]) + dot(tok[d, rows:], l2[slabs - 1, lanes, :])
            h = a / (1.0 + jnp.exp(-a))
            hid[d, lanes] = h.astype(BF16)
            r2[t, lanes, :] = h.T.astype(BF16)
            return 0

        lax.fori_loop(0, rows // width, one, 0)

    for p in range(2):
        own_in(p).wait()
    for j in range(rows // width):
        up_a(j).wait()
        up_b(j).wait()
    for p in range(2):
        t_core(p).wait_recv()
        hidden(p, yl)
    for c in range(slabs):
        w_in(c).wait()
        t_in(c).wait()
    for p in range(2):
        t_mate(p).wait_recv()
        t_fwd(p).start()
        t_fwd(p).wait_recv()
        hidden(p, 1 - yl)
    for p in range(2):
        t_fwd(p).wait_send()

    scale = ff ** -0.5

    def prx(c):
        return r2.at[4 + c // 3, pl.ds(pl.multiple_of((c % 3) * 2 * trow, trow), 2 * trow)]

    def psend(c):
        return tok.at[pl.ds(0, 2 * trow), pl.ds(pl.multiple_of(c * width, width), width)]

    def qsend(c):
        return tok.at[pl.ds(2 * trow, 2 * trow), pl.ds(pl.multiple_of(c * width, width), width)]

    def c_p(c):
        return send(psend(c), prx(c), ps.at[c], pr.at[c], core)

    def c_q(c):
        return send(qsend(c), qrx.at[c], qs.at[c], qr.at[c], mate)

    def c_r(c):
        return send(qrx.at[c], rrx.at[c], rs.at[c], rr.at[c], core)

    def item(i):
        c, o = (i % chunks) // 2, i % 2
        d = pl.ds(o * cr, cr)
        return c, d

    def items(i):
        c, d = item(i)
        src, dl, dr = (s, l1, r1) if i < chunks else (l1, l2, r2)
        return (send(src.at[c, d], dl.at[c, d], gs.at[0, i], gr.at[0, i], right),
                send(src.at[c, d], dr.at[c, d], gs.at[1, i], gr.at[1, i], left))

    def s_items(c):
        for o in range(2):
            d = pl.ds(o * cr, cr)
            i = 2 * c + o
            send(s.at[c, d], l1.at[c, d], gs.at[0, i], gr.at[0, i], right).start()
            send(s.at[c, d], r1.at[c, d], gs.at[1, i], gr.at[1, i], left).start()

    row_core = lax.broadcasted_iota(jnp.int32, (trow, width), 0) // tp

    def stage_a(c):
        lanes = pl.ds(pl.multiple_of(c * width, width), width)

        def one(i, _):
            w, chip = i // 2, i % 2
            a = dot(hid[pl.ds(pl.multiple_of(i * trow, trow), trow), :], s[c]) * scale
            p = w + e - 2 * w * e
            y = piece[c, pl.ds(pl.multiple_of(p * tp, tp), tp), :].astype(F32)
            y = jnp.concatenate([y, y], axis=0)
            keep = jnp.logical_and(row_core == e, chip == yl)
            a = a - jnp.where(keep, y, 0.0)

            @pl.when(w == 0)
            def _():
                pown[pl.ds(pl.multiple_of(chip * trow, trow), trow), :] = a

            @pl.when(w == 1)
            def _():
                tok[pl.ds(pl.multiple_of(chip * trow, trow), trow), lanes] = a.astype(BF16)

            return 0

        lax.fori_loop(0, 4, one, 0)
        c_p(c).start()

    def stage_b(c):
        c_p(c).wait_recv()
        lanes = pl.ds(pl.multiple_of(c * width, width), width)

        def one(i, _):
            o = pl.ds(pl.multiple_of(i * 64, 64), 64)
            other = r2[4 + c // 3, pl.ds(pl.multiple_of((c % 3) * 2 * trow + i * 64, 64), 64), :]
            tok[pl.ds(pl.multiple_of(2 * trow + i * 64, 64), 64), lanes] = (pown[o, :] + other.astype(F32)).astype(BF16)
            return 0

        lax.fori_loop(0, 2 * trow // 64, one, 0)
        c_q(c).start()

    def stage_c(c):
        c_q(c).wait_recv()
        lanes = pl.ds(pl.multiple_of(c * width, width), width)

        def one(i, _):
            o = pl.ds(pl.multiple_of(i * 64, 64), 64)
            mine = tok[pl.ds(pl.multiple_of(2 * trow + i * 64, 64), 64), lanes]
            qrx[c, o, :] = (qrx[c, o, :].astype(F32) + mine.astype(F32)).astype(BF16)
            return 0

        lax.fori_loop(0, 2 * trow // 64, one, 0)
        c_r(c).start()

    def stage_d(c):
        c_r(c).wait_recv()

        def one(i, _):
            d = pl.ds(pl.multiple_of(i * width, width), width)
            g = dot(r2[0, d, :], qrx[c, :trow, :])
            g += dot(r2[1, d, :], qrx[c, trow:, :])
            g += dot(r2[2, d, :], rrx[c, :trow, :])
            g += dot(r2[3, d, :], rrx[c, trow:, :])
            s[c, d, :] = (s[c, d, :].astype(F32) - (LEARN_RATE * scale) * g).astype(BF16)
            return 0

        lax.fori_loop(0, rows // width, one, 0)
        pl.when(c < EARLY // 2)(lambda: s_items(c))

    def k1(i, _):
        pl.when(jnp.logical_and(i >= 1, i <= slabs))(lambda: stage_b(i - 1))
        pl.when(i >= 2)(lambda: stage_c(i - 2))
        pl.when(i < slabs)(lambda: stage_a(i))
        pl.when(i >= 2)(lambda: stage_d(i - 2))
        return 0

    lax.fori_loop(0, slabs + 2, k1, 0)

    BR = 64

    def over(i, body):
        c, _ = item(i)
        lo = (i % 2) * cr

        def one(k, _):
            body(c, pl.ds(pl.multiple_of(lo + k * BR, BR), BR))
            return 0

        lax.fori_loop(0, cr // BR, one, 0)

    def first(i):
        def body(c, d):
            a = s[c, d, :].astype(F32)
            p = l1[c, d, :].astype(F32)
            q = r1[c, d, :].astype(F32)
            l1[c, d, :] = (m[0][0] * a + m[0][1] * p + m[0][2] * q).astype(BF16)
            r1[c, d, :] = (wb * a + wl * p + wr * q).astype(BF16)
        over(i, body)

    def second(i):
        def body(c, d):
            a = l1[c, d, :].astype(F32)
            p = l2[c, d, :].astype(F32)
            q = r2[c, d, :].astype(F32)
            l2[c, d, :] = (m[1][0] * a + m[1][1] * p + m[1][2] * q).astype(BF16)
        over(i, body)

    def o_copy(i):
        c, d = item(i)
        return pltpu.make_async_copy(l2.at[c, d], out.at[0, d, pl.ds(c * width, width)], os.at[i])

    def last(i):
        def body(c, d):
            l2[c, d, :] = (l2[c, d, :].astype(F32) - avg[c, d, :].astype(F32)).astype(BF16)
        over(i, body)
        o_copy(i).start()

    def own(g, xx, lo, size):
        return (pl.ds(g * per, per), pl.ds(pl.multiple_of(xx * quarter + lo, 32), size), slice(None))

    def a_rs(g, j):
        xx = (x + j) % 4
        return send(r1.at[own(g, xx, 0, quarter)], rsx.at[j - 1, pl.ds(g * per, per)],
                    xs.at[g, j - 1], xr.at[g, j - 1], at(xx, yh, z))

    def a_y(g):
        return send(piece.at[pl.ds(g * per, per), pl.ds(pl.multiple_of((1 - yh) * half, 32), half)],
                    yrx.at[pl.ds(g * per, per)], ys.at[0, g], yr.at[0, g], ydev)

    def a_z(g):
        return send(piece.at[pl.ds(g * per, per), pl.ds(pl.multiple_of(yh * half, 32), half)],
                    zrx.at[pl.ds(g * per, per)], zs.at[0, g], zr.at[0, g], zdev)

    def a_yg(g):
        ref = avg.at[own(g, x, yh * half, half)]
        return send(ref, ref, ys.at[1, g], yr.at[1, g], ydev)

    around = [g < groups - 1 for g in range(groups)]

    def a_zb(g):
        to = at(x, yh, jnp.where(z == 1, 0, jnp.where(z == 2, 3, 3 - z)))
        if around[g]:
            ref = avg.at[own(g, x, jnp.where(z <= 1, 0, half), half)]
        else:
            ref = avg.at[own(g, x, 0, quarter)]
        return send(ref, ref, zs.at[1, g], zr.at[1, g], to)

    def a_zf(g):
        ref = avg.at[own(g, x, jnp.where(z <= 1, 0, half), half)]
        return send(ref, ref, zs.at[2, g], zr.at[2, g], zdev)

    def a_x(g, k):
        if k == 0:
            ref, to = avg.at[own(g, x, 0, quarter)], xp
        elif k == 1:
            ref, to = avg.at[own(g, x, 0, quarter)], xm
        elif k == 2:
            ref, to = avg.at[own(g, (x + 3) % 4, 0, half)], xp
        else:
            ref, to = avg.at[own(g, (x + 1) % 4, half, half)], xm
        return send(ref, ref, as_.at[g, k], ar.at[g, k], to)

    when = lambda cond, f: pl.when(cond)(f)

    def e_rs(g):
        def go():
            for j in (1, 2, 3):
                a_rs(g, j).start()
        when(inner, go)

    def e_y(g):
        def go():
            for j in (1, 2, 3):
                a_rs(g, j).wait_recv()
            for cc in range(per):
                c = g * per + cc

                def one(i, _):
                    d = pl.ds(pl.multiple_of(i * 64, 64), 64)
                    o = pl.ds(pl.multiple_of(x * quarter + i * 64, 64), 64)
                    t = r1[c, o, :].astype(F32)
                    for j in range(3):
                        t += rsx[j, c, d, :].astype(F32)
                    piece[c, d, :] = t.astype(BF16)
                    return 0

                lax.fori_loop(0, quarter // 64, one, 0)
            a_y(g).start()
        when(inner, go)

    def add_half(g, other, final):
        for cc in range(per):
            c = g * per + cc

            def one(i, _):
                d = pl.ds(pl.multiple_of(i * 32, 32), 32)
                o = pl.ds(pl.multiple_of(yh * half + i * 32, 32), 32)
                t = piece[c, o, :].astype(F32) + other[c, d, :].astype(F32)
                if final:
                    p = pl.ds(pl.multiple_of(x * quarter + yh * half + i * 32, 32), 32)
                    avg[c, p, :] = (t * (1.0 / NW)).astype(BF16)
                else:
                    piece[c, o, :] = t.astype(BF16)
                return 0

            lax.fori_loop(0, half // 32, one, 0)

    def e_z(g):
        def go():
            a_y(g).wait_recv()
            add_half(g, yrx, False)
            a_z(g).start()
        when(inner, go)

    def e_yg(g):
        def go():
            a_z(g).wait_recv()
            add_half(g, zrx, True)
            a_yg(g).start()
        when(inner, go)

    def e_zb(g):
        def go():
            a_yg(g).wait_recv()
            a_zb(g).start()
        when(inner, go)

    def e_zf(g):
        def go():
            a_zb(g).wait_recv()
            a_zf(g).start()
        when(outer, go)

    def e_x0(g):
        when(outer, lambda: (a_zf if around[g] else a_zb)(g).wait_recv())
        a_x(g, 0).start()
        a_x(g, 1).start()

    def e_x1(g):
        a_x(g, 0).wait_recv()
        a_x(g, 1).wait_recv()
        a_x(g, 2).start()
        a_x(g, 3).start()

    def e_x2(g):
        a_x(g, 2).wait_recv()
        a_x(g, 3).wait_recv()

    stages = (e_rs, e_y, e_z, e_yg, e_zb, e_zf, e_x0, e_x1, e_x2)
    plan = ((3, 5, 6, 10, 11, 14, 17, 19, 20),
            (7, 9, 10, 13, 14, 17, 20, 22, 23),
            (11, 13, 14, 17, 18, 21, 24, 26, 27),
            (15, 17, 18, 21, 22, None, 25, 27, 28))
    events = {}
    for g in range(groups):
        for f, slot in zip(stages, plan[g]):
            if slot is not None:
                events.setdefault(slot, []).append((f, g))

    ready = []
    for slot in range(2 * chunks):
        for cp in items(slot):
            cp.wait_recv()
        if slot < chunks:
            first(slot)
        else:
            second(slot)
        if EARLY <= slot + DEPTH < 2 * chunks:
            for cp in items(slot + DEPTH):
                cp.start()
        for f, g in events.get(slot, ()):
            f(g)
        if slot >= chunks:
            ready.append(slot)
            for i in [i for i in ready if plan[(i - chunks) // (2 * per)][-1] <= slot]:
                last(i)
                ready.remove(i)
    assert not ready

    for p in range(2):
        t_core(p).wait_send()
        t_mate(p).wait_send()
    for c in range(slabs):
        c_p(c).wait_send()
        c_q(c).wait_send()
        c_r(c).wait_send()
    for i in range(2 * chunks):
        for cp in items(i):
            cp.wait_send()
    for g in range(groups):
        def drain():
            for j in (1, 2, 3):
                a_rs(g, j).wait_send()
            for f in (a_y, a_z, a_yg, a_zb):
                f(g).wait_send()
        when(inner, drain)
        if around[g]:
            when(outer, lambda: a_zf(g).wait_send())
        for k in range(4):
            a_x(g, k).wait_send()
    for i in range(chunks, 2 * chunks):
        o_copy(i).wait()


def body(tokens, targets, up_weight, down_weight, mix_numer):
    rows, dim = down_weight.shape[1:]
    slabs = 8
    width = dim // slabs
    trow = tokens.shape[0]
    D = pltpu.SemaphoreType.DMA
    vm = lambda *shape: pltpu.VMEM(shape, BF16)
    any_ = pl.BlockSpec(memory_space=pl.ANY)
    return pl.pallas_call(
        kernel,
        out_shape=jax.ShapeDtypeStruct(down_weight.shape, BF16),
        in_specs=[pl.BlockSpec(memory_space=pltpu.SMEM)] + [any_] * 4,
        out_specs=any_,
        scratch_shapes=[vm(slabs, rows, width)] * 6 + [
            vm(3, slabs, rows // 4, width), vm(slabs, rows // 4, width),
            vm(slabs, rows // 8, width), vm(slabs, rows // 8, width),
            vm(4 * trow, dim), vm(4 * trow, rows),
            vm(slabs, 2 * trow, width), vm(slabs, 2 * trow, width),
            pltpu.VMEM((2 * trow, width), F32),
            D((5, slabs)), D((3, 2)), D((3, 2)),
            D((slabs,)), D((slabs,)), D((slabs,)), D((slabs,)), D((slabs,)), D((slabs,)),
            D((2, 4 * slabs)), D((2, 4 * slabs)), D((4, 3)), D((4, 3)), D((4, 4)), D((4, 4)),
            D((2, 4)), D((2, 4)), D((3, 4)), D((3, 4)), D((4 * slabs,)),
        ],
        compiler_params=pltpu.CompilerParams(
            collective_id=0, has_side_effects=True, vmem_limit_bytes=67_043_328),
        name="gossip",
    )(mix_numer.reshape(-1), tokens, targets, up_weight, down_weight)


def solution(mesh):
    in_specs = (P(("blk", "shard"), None), P(("blk", "shard"), None), P(None, "shard"), P("blk", "shard", None), P())
    return jax.shard_map(body, mesh=mesh, in_specs=in_specs, out_specs=P("blk", "shard", None), check_vma=False)
```

time: 597 us -> 616 us (1.032)
  Pallas kernels: 366 us -> 606 us
  waiting for transfers between devices: 141 us -> 0 us
  matrix products: 38.1 us -> 0 us
  local copies, waits for them, and re-layouts: 31.3 us -> 9 us
  between operations: 13.1 us -> 0.01 us
    pallas_call x1, Pallas kernels: 366 us -> 606 us  [body(): pl.pallas_call(kernel, out_shape=jax.ShapeDtypeStruct(down_weight.shape,...]
    all_gather x2 -> x0, waiting for transfers between devices: 94 us -> none  [the longest x1 47.9 us: body(): lax.all_gather(tokens, 'shard', axis=0, tiled=True)]
    reduce_scatter x1 -> x0, waiting for transfers between devices: 46.7 us -> none  [body(): lax.psum_scatter((jnp.dot(hidden, weight, preferred_element_type=F32) * o...]
    dot_general x3 -> x0, matrix products: 38.1 us -> none  [the longest x1 14.9 us: body(): lax.dot_general(hidden, lax.all_gather(resid, 'shard', axis=0, tiled=True...]
    reshape x2 -> x1, local copies, waits for them, and re-layouts: 10.7 us -> 0.7 us  [body(): mix_numer.reshape(-1)]
    convert_element_type x1 -> x0, local copies, waits for them, and re-layouts: 9.93 us -> none  [body(): stepped = (weight.astype(F32) - LEARN_RATE * grad * out_scale).astype(BF16)]
  transfers between devices with their start and end apart: 3 -> 0, of which waited for: 3 -> 0; matrix products, arithmetic and copies ran while one was open for 0% -> 0% of each run, Pallas kernels for 0% -> 0%
where the time goes in v2:
time: 616 us; the launch traced here: 615 us
  Pallas kernels  606 us (98%)
  local copies, waits for them, and re-layouts  9 us (1%)
    pallas_call x1, Pallas kernels, body(): pl.pallas_call(kernel, out_shape=jax.ShapeDtypeStruct(down_weight.shape,...  606 us

profile of v2, /device:TPU:120, one launch (start us, length us, event | category | flops | bytes accessed | tf_op | source)
XLA Modules:
  0.0 615.5 jit_solution(17840696155894665323)
XLA Ops:
  0.0 0.8 copy.6
  0.8 0.7 reshape.3.numer
  1.5 606.4 %gossip.1 = bf16[1,1792,2048]{2,1,0:T(8,128)(2,1)} custom-call(s32[192]{0:T(256)} %reshape.3.numer, bf16[256,2048]{1,0:T(8,128)(2,1)} %tokens.1, bf16[256,2048]{1,0:T(8,128)(2,1)} %targets.1, bf16[2048,1792]{1,0:T(8,128)(2,1)} %up.1, bf16[1,1792,2048]{2,1,0:T(8,128)(2,1)} %weight.1), custom_call_target="tpu_custom_call" | custom-call | tf_op jit(solution)/shard_map/gossip/pallas_call | solution.py:501
  607.9 7.5 %copy.8 = bf16[1,1792,2048]{2,1,0:T(8,128)(2,1)} copy(bf16[1,1792,2048]{2,1,0:T(8,128)(2,1)} %gossip.1) | data formatting | bytes 14680064

commit v3 on v2

--- a/solution.py
+++ b/solution.py
@@ -1,3 +1,5 @@
+import functools
+
 import jax
 import jax.numpy as jnp
 from jax import lax
@@ -8,8 +10,7 @@
 MESH = pl.DeviceIdType.MESH
 LEARN_RATE = 2.0
 NW = 32
-DEPTH = 2
-EARLY = 10
+WRAP_DEPTH = 2
 F32 = jnp.float32
 BF16 = jnp.bfloat16
 
@@ -43,6 +44,9 @@
     xp, xm = at((x + 1) % 4, yh, z), at((x + 3) % 4, yh, z)
     inner = jnp.logical_or(z == 1, z == 2)
     outer = jnp.logical_or(z == 0, z == 3)
+    loaded = jnp.logical_or(jnp.logical_and(z == 0, yh == 0), jnp.logical_and(z == 3, yh == 1))
+    plain = jnp.logical_and(outer, jnp.logical_not(loaded))
+    way = jnp.where(z == 0, 1, 3)
 
     def send(src, dst, ss, rsem, dev):
         return pltpu.make_async_remote_copy(src, dst, ss, rsem, device_id=dev, device_id_type=MESH)
@@ -130,41 +134,20 @@
 
         lax.fori_loop(0, rows // width, one, 0)
 
-    for p in range(2):
-        own_in(p).wait()
-    for j in range(rows // width):
-        up_a(j).wait()
-        up_b(j).wait()
-    for p in range(2):
-        t_core(p).wait_recv()
-        hidden(p, yl)
-    for c in range(slabs):
-        w_in(c).wait()
-        t_in(c).wait()
-    for p in range(2):
-        t_mate(p).wait_recv()
-        t_fwd(p).start()
-        t_fwd(p).wait_recv()
-        hidden(p, 1 - yl)
-    for p in range(2):
-        t_fwd(p).wait_send()
-
     scale = ff ** -0.5
 
-    def prx(c):
-        return r2.at[4 + c // 3, pl.ds(pl.multiple_of((c % 3) * 2 * trow, trow), 2 * trow)]
-
-    def psend(c):
-        return tok.at[pl.ds(0, 2 * trow), pl.ds(pl.multiple_of(c * width, width), width)]
-
-    def qsend(c):
-        return tok.at[pl.ds(2 * trow, 2 * trow), pl.ds(pl.multiple_of(c * width, width), width)]
-
-    def c_p(c):
-        return send(psend(c), prx(c), ps.at[c], pr.at[c], core)
-
-    def c_q(c):
-        return send(qsend(c), qrx.at[c], qs.at[c], qr.at[c], mate)
+    def lanes_of(c):
+        return pl.ds(pl.multiple_of(c * width, width), width)
+
+    def block(lo, i=0, size=None):
+        return pl.ds(pl.multiple_of(lo * trow + i, 64), trow if size is None else size)
+
+    def c_p(c, chip):
+        return send(tok.at[block(2 + chip), lanes_of(c)], r2.at[4 + c // 3, block((c % 3) * 2 + chip)],
+                    ps.at[c, chip], pr.at[c, chip], core)
+
+    def c_q(c, chip):
+        return send(tok.at[block(chip), lanes_of(c)], qrx.at[c, block(chip)], qs.at[c, chip], qr.at[c, chip], mate)
 
     def c_r(c):
         return send(qrx.at[c], rrx.at[c], rs.at[c], rr.at[c], core)
@@ -177,64 +160,80 @@
     def items(i):
         c, d = item(i)
         src, dl, dr = (s, l1, r1) if i < chunks else (l1, l2, r2)
-        return (send(src.at[c, d], dl.at[c, d], gs.at[0, i], gr.at[0, i], right),
-                send(src.at[c, d], dr.at[c, d], gs.at[1, i], gr.at[1, i], left))
-
-    def s_items(c):
-        for o in range(2):
-            d = pl.ds(o * cr, cr)
-            i = 2 * c + o
-            send(s.at[c, d], l1.at[c, d], gs.at[0, i], gr.at[0, i], right).start()
-            send(s.at[c, d], r1.at[c, d], gs.at[1, i], gr.at[1, i], left).start()
+        return (lambda: send(src.at[c, d], dl.at[c, d], gs.at[0, i], gr.at[0, i], right),
+                lambda: send(src.at[c, d], dr.at[c, d], gs.at[1, i], gr.at[1, i], left))
+
+    def right_item(c, o, i):
+        d = pl.ds(o * cr if isinstance(o, int) else pl.multiple_of(o * cr, cr), cr)
+        return send(s.at[c, d], l1.at[c, d], gs.at[0, i], gr.at[0, i], right)
+
+    def left_item(c, o, i):
+        d = pl.ds(o * cr if isinstance(o, int) else pl.multiple_of(o * cr, cr), cr)
+        return send(s.at[c, d], r1.at[c, d], gs.at[1, i], gr.at[1, i], left)
+
+    def early(c):
+        @pl.when(z == 0)
+        def _():
+            for o in range(2):
+                right_item(c, o, 2 * c + o).start()
+
+        @pl.when(z == 3)
+        def _():
+            for o in range(2):
+                left_item(c, o, 2 * c + o).start()
+
+        @pl.when(inner)
+        def _():
+            right_item(c // 2, c % 2, c).start()
+            left_item(c // 2, c % 2, c).start()
 
     row_core = lax.broadcasted_iota(jnp.int32, (trow, width), 0) // tp
 
-    def stage_a(c):
-        lanes = pl.ds(pl.multiple_of(c * width, width), width)
-
-        def one(i, _):
-            w, chip = i // 2, i % 2
-            a = dot(hid[pl.ds(pl.multiple_of(i * trow, trow), trow), :], s[c]) * scale
+    def stage_a(c, chip):
+        lanes = lanes_of(c)
+
+        def one(w, _):
+            rows_at = block(w * 2 + chip)
+            a = dot(hid[rows_at, :], s[c]) * scale
             p = w + e - 2 * w * e
             y = piece[c, pl.ds(pl.multiple_of(p * tp, tp), tp), :].astype(F32)
             y = jnp.concatenate([y, y], axis=0)
-            keep = jnp.logical_and(row_core == e, chip == yl)
-            a = a - jnp.where(keep, y, 0.0)
+            a = a - jnp.where(jnp.logical_and(row_core == e, chip == yl), y, 0.0)
 
             @pl.when(w == 0)
             def _():
-                pown[pl.ds(pl.multiple_of(chip * trow, trow), trow), :] = a
+                pown[...] = a
 
             @pl.when(w == 1)
             def _():
-                tok[pl.ds(pl.multiple_of(chip * trow, trow), trow), lanes] = a.astype(BF16)
+                tok[rows_at, lanes] = a.astype(BF16)
 
             return 0
 
-        lax.fori_loop(0, 4, one, 0)
-        c_p(c).start()
-
-    def stage_b(c):
-        c_p(c).wait_recv()
-        lanes = pl.ds(pl.multiple_of(c * width, width), width)
+        lax.fori_loop(0, 2, one, 0)
+        c_p(c, chip).start()
+
+    def stage_b(c, chip):
+        c_p(c, chip).wait_recv()
+        lanes = lanes_of(c)
+
+        def one(i, _):
+            other = r2[4 + c // 3, block((c % 3) * 2 + chip, i * 64, 64), :]
+            mine = pown[pl.ds(pl.multiple_of(i * 64, 64), 64), :]
+            tok[block(chip, i * 64, 64), lanes] = (mine + other.astype(F32)).astype(BF16)
+            return 0
+
+        lax.fori_loop(0, trow // 64, one, 0)
+        c_q(c, chip).start()
+
+    def stage_c(c):
+        for chip in range(2):
+            c_q(c, chip).wait_recv()
+        lanes = lanes_of(c)
 
         def one(i, _):
             o = pl.ds(pl.multiple_of(i * 64, 64), 64)
-            other = r2[4 + c // 3, pl.ds(pl.multiple_of((c % 3) * 2 * trow + i * 64, 64), 64), :]
-            tok[pl.ds(pl.multiple_of(2 * trow + i * 64, 64), 64), lanes] = (pown[o, :] + other.astype(F32)).astype(BF16)
-            return 0
-
-        lax.fori_loop(0, 2 * trow // 64, one, 0)
-        c_q(c).start()
-
-    def stage_c(c):
-        c_q(c).wait_recv()
-        lanes = pl.ds(pl.multiple_of(c * width, width), width)
-
-        def one(i, _):
-            o = pl.ds(pl.multiple_of(i * 64, 64), 64)
-            mine = tok[pl.ds(pl.multiple_of(2 * trow + i * 64, 64), 64), lanes]
-            qrx[c, o, :] = (qrx[c, o, :].astype(F32) + mine.astype(F32)).astype(BF16)
+            qrx[c, o, :] = (qrx[c, o, :].astype(F32) + tok[o, lanes].astype(F32)).astype(BF16)
             return 0
 
         lax.fori_loop(0, 2 * trow // 64, one, 0)
@@ -253,16 +252,42 @@
             return 0
 
         lax.fori_loop(0, rows // width, one, 0)
-        pl.when(c < EARLY // 2)(lambda: s_items(c))
-
-    def k1(i, _):
-        pl.when(jnp.logical_and(i >= 1, i <= slabs))(lambda: stage_b(i - 1))
+        early(c)
+
+    for p in range(2):
+        own_in(p).wait()
+    for j in range(rows // width):
+        up_a(j).wait()
+        up_b(j).wait()
+    for p in range(2):
+        t_core(p).wait_recv()
+        hidden(p, yl)
+    for c in range(slabs):
+        w_in(c).wait()
+        t_in(c).wait()
+
+    def own_step(i, _):
+        pl.when(i >= 1)(lambda: stage_b(i - 1, yl))
+        pl.when(i < slabs)(lambda: stage_a(i, yl))
+        return 0
+
+    lax.fori_loop(0, slabs + 1, own_step, 0)
+    for p in range(2):
+        t_mate(p).wait_recv()
+        t_fwd(p).start()
+        t_fwd(p).wait_recv()
+        hidden(p, 1 - yl)
+    for p in range(2):
+        t_fwd(p).wait_send()
+
+    def other_step(i, _):
+        pl.when(jnp.logical_and(i >= 1, i <= slabs))(lambda: stage_b(i - 1, 1 - yl))
         pl.when(i >= 2)(lambda: stage_c(i - 2))
-        pl.when(i < slabs)(lambda: stage_a(i))
+        pl.when(i < slabs)(lambda: stage_a(i, 1 - yl))
         pl.when(i >= 2)(lambda: stage_d(i - 2))
         return 0
 
-    lax.fori_loop(0, slabs + 2, k1, 0)
+    lax.fori_loop(0, slabs + 2, other_step, 0)
 
     BR = 64
 
@@ -348,33 +373,33 @@
             ref, to = avg.at[own(g, (x + 1) % 4, half, half)], xm
         return send(ref, ref, as_.at[g, k], ar.at[g, k], to)
 
-    when = lambda cond, f: pl.when(cond)(f)
+    def when(cond, *fs):
+        @pl.when(cond)
+        def _():
+            for f in fs:
+                f()
 
     def e_rs(g):
-        def go():
-            for j in (1, 2, 3):
-                a_rs(g, j).start()
-        when(inner, go)
+        for j in (1, 2, 3):
+            a_rs(g, j).start()
 
     def e_y(g):
-        def go():
-            for j in (1, 2, 3):
-                a_rs(g, j).wait_recv()
-            for cc in range(per):
-                c = g * per + cc
-
-                def one(i, _):
-                    d = pl.ds(pl.multiple_of(i * 64, 64), 64)
-                    o = pl.ds(pl.multiple_of(x * quarter + i * 64, 64), 64)
-                    t = r1[c, o, :].astype(F32)
-                    for j in range(3):
-                        t += rsx[j, c, d, :].astype(F32)
-                    piece[c, d, :] = t.astype(BF16)
-                    return 0
-
-                lax.fori_loop(0, quarter // 64, one, 0)
-            a_y(g).start()
-        when(inner, go)
+        for j in (1, 2, 3):
+            a_rs(g, j).wait_recv()
+        for cc in range(per):
+            c = g * per + cc
+
+            def one(i, _):
+                d = pl.ds(pl.multiple_of(i * 64, 64), 64)
+                o = pl.ds(pl.multiple_of(x * quarter + i * 64, 64), 64)
+                t = r1[c, o, :].astype(F32)
+                for j in range(3):
+                    t += rsx[j, c, d, :].astype(F32)
+                piece[c, d, :] = t.astype(BF16)
+                return 0
+
+            lax.fori_loop(0, quarter // 64, one, 0)
+        a_y(g).start()
 
     def add_half(g, other, final):
         for cc in range(per):
@@ -394,35 +419,30 @@
             lax.fori_loop(0, half // 32, one, 0)
 
     def e_z(g):
-        def go():
-            a_y(g).wait_recv()
-            add_half(g, yrx, False)
-            a_z(g).start()
-        when(inner, go)
+        a_y(g).wait_recv()
+        add_half(g, yrx, False)
+        a_z(g).start()
 
     def e_yg(g):
-        def go():
-            a_z(g).wait_recv()
-            add_half(g, zrx, True)
-            a_yg(g).start()
-        when(inner, go)
+        a_z(g).wait_recv()
+        add_half(g, zrx, True)
+        a_yg(g).start()
 
     def e_zb(g):
-        def go():
-            a_yg(g).wait_recv()
-            a_zb(g).start()
-        when(inner, go)
+        a_yg(g).wait_recv()
+        a_zb(g).start()
 
     def e_zf(g):
-        def go():
-            a_zb(g).wait_recv()
-            a_zf(g).start()
-        when(outer, go)
+        a_zb(g).wait_recv()
+        a_zf(g).start()
 
     def e_x0(g):
-        when(outer, lambda: (a_zf if around[g] else a_zb)(g).wait_recv())
         a_x(g, 0).start()
         a_x(g, 1).start()
+
+    def e_x0_out(g):
+        (a_zf if around[g] else a_zb)(g).wait_recv()
+        e_x0(g)
 
     def e_x1(g):
         a_x(g, 0).wait_recv()
@@ -434,33 +454,76 @@
         a_x(g, 2).wait_recv()
         a_x(g, 3).wait_recv()
 
-    stages = (e_rs, e_y, e_z, e_yg, e_zb, e_zf, e_x0, e_x1, e_x2)
-    plan = ((3, 5, 6, 10, 11, 14, 17, 19, 20),
-            (7, 9, 10, 13, 14, 17, 20, 22, 23),
-            (11, 13, 14, 17, 18, 21, 24, 26, 27),
-            (15, 17, 18, 21, 22, None, 25, 27, 28))
-    events = {}
+    def a_way(g, k):
+        ref = avg.at[own(g, (x + k * (4 - way)) % 4, 0, quarter)]
+        return send(ref, ref, as_.at[g, k], ar.at[g, k], at((x + way) % 4, yh, z))
+
+    def e_w0(g):
+        (a_zf if around[g] else a_zb)(g).wait_recv()
+        a_way(g, 0).start()
+
+    def e_w(k, g):
+        a_way(g, k).wait_recv()
+        if k < 2:
+            a_way(g, k + 1).start()
+
+    stages = (e_rs, e_y, e_z, e_yg, e_zb, e_x0, e_x1, e_x2)
+    plan_in = ((3, 5, 6, 10, 11, 12, 14, 16),
+               (7, 9, 10, 14, 15, 16, 18, 20),
+               (11, 13, 14, 18, 19, 20, 22, 24),
+               (15, 17, 18, 22, 23, 24, 26, 28))
+    plan_out = ((11, 13, 15, 17), (15, 17, 19, 21), (19, 21, 23, 25), (None, 24, 26, 28))
+    plan_way = ((11, 13, 15, 17, 19), (15, 17, 19, 21, 23), (19, 21, 23, 25, 27), (None, 24, 26, 28, 30))
+    ways = [functools.partial(e_w, k) for k in range(3)]
+    inside, outside, special = {}, {}, {}
     for g in range(groups):
-        for f, slot in zip(stages, plan[g]):
+        for f, slot in zip(stages, plan_in[g]):
+            inside.setdefault(slot, []).append((f, g))
+        for f, slot in zip((e_zf, e_x0_out, e_x1, e_x2), plan_out[g]):
             if slot is not None:
-                events.setdefault(slot, []).append((f, g))
-
+                outside.setdefault(slot, []).append((f, g))
+        for f, slot in zip((e_zf, e_w0, *ways), plan_way[g]):
+            if slot is not None:
+                special.setdefault(slot, []).append((f, g))
+    jit, wrap, bulk = {}, {}, {}
+    for i in range(slabs, 2 * chunks):
+        jit.setdefault(i - 3 if i < chunks else max(i - 3, chunks - 2), []).append(i)
+    for i in range(WRAP_DEPTH, 2 * chunks):
+        wrap.setdefault(i - WRAP_DEPTH, []).append(i)
+    for i in range(chunks, 2 * chunks):
+        bulk.setdefault(max(i - chunks, slabs), []).append(i)
+
+    def put(direction, those):
+        for i in those:
+            items(i)[direction]().start()
+
+    def issue(slot):
+        if slot in jit:
+            when(inner, lambda: put(0, jit[slot]), lambda: put(1, jit[slot]))
+        if slot in wrap or slot in bulk:
+            when(z == 3, lambda: put(0, wrap.get(slot, ())), lambda: put(1, bulk.get(slot, ())))
+            when(z == 0, lambda: put(1, wrap.get(slot, ())), lambda: put(0, bulk.get(slot, ())))
+
+    when(z == 3, lambda: put(0, range(WRAP_DEPTH)))
+    when(z == 0, lambda: put(1, range(WRAP_DEPTH)))
     ready = []
     for slot in range(2 * chunks):
         for cp in items(slot):
-            cp.wait_recv()
+            cp().wait_recv()
         if slot < chunks:
             first(slot)
         else:
             second(slot)
-        if EARLY <= slot + DEPTH < 2 * chunks:
-            for cp in items(slot + DEPTH):
-                cp.start()
-        for f, g in events.get(slot, ()):
-            f(g)
+        issue(slot)
+        if slot in inside:
+            when(inner, *[functools.partial(f, g) for f, g in inside[slot]])
+        if slot in outside:
+            when(plain, *[functools.partial(f, g) for f, g in outside[slot]])
+        if slot in special:
+            when(loaded, *[functools.partial(f, g) for f, g in special[slot]])
         if slot >= chunks:
             ready.append(slot)
-            for i in [i for i in ready if plan[(i - chunks) // (2 * per)][-1] <= slot]:
+            for i in [i for i in ready if max(p[(i - chunks) // (2 * per)][-1] for p in (plan_in, plan_out, plan_way)) <= slot]:
                 last(i)
                 ready.remove(i)
     assert not ready
@@ -469,12 +532,13 @@
         t_core(p).wait_send()
         t_mate(p).wait_send()
     for c in range(slabs):
-        c_p(c).wait_send()
-        c_q(c).wait_send()
+        for chip in range(2):
+            c_p(c, chip).wait_send()
+            c_q(c, chip).wait_send()
         c_r(c).wait_send()
     for i in range(2 * chunks):
         for cp in items(i):
-            cp.wait_send()
+            cp().wait_send()
     for g in range(groups):
         def drain():
             for j in (1, 2, 3):
@@ -484,8 +548,8 @@
         when(inner, drain)
         if around[g]:
             when(outer, lambda: a_zf(g).wait_send())
-        for k in range(4):
-            a_x(g, k).wait_send()
+        when(loaded, *[a_way(g, k).wait_send for k in range(3)])
+        when(jnp.logical_not(loaded), *[a_x(g, k).wait_send for k in range(4)])
     for i in range(chunks, 2 * chunks):
         o_copy(i).wait()
 
@@ -508,9 +572,9 @@
             vm(slabs, rows // 8, width), vm(slabs, rows // 8, width),
             vm(4 * trow, dim), vm(4 * trow, rows),
             vm(slabs, 2 * trow, width), vm(slabs, 2 * trow, width),
-            pltpu.VMEM((2 * trow, width), F32),
+            pltpu.VMEM((trow, width), F32),
             D((5, slabs)), D((3, 2)), D((3, 2)),
-            D((slabs,)), D((slabs,)), D((slabs,)), D((slabs,)), D((slabs,)), D((slabs,)),
+            D((slabs, 2)), D((slabs, 2)), D((slabs, 2)), D((slabs, 2)), D((slabs,)), D((slabs,)),
             D((2, 4 * slabs)), D((2, 4 * slabs)), D((4, 3)), D((4, 3)), D((4, 4)), D((4, 4)),
             D((2, 4)), D((2, 4)), D((3, 4)), D((3, 4)), D((4 * slabs,)),
         ],

time: 616 us -> 457 us (0.74); the launches traced: 615 us -> 448 us
  Pallas kernels: 606 us -> 439 us
    pallas_call x1, Pallas kernels: 606 us -> 439 us  [body(): pl.pallas_call(kernel, out_shape=jax.ShapeDtypeStruct(down_weight.shape,...]
where the time goes in v3:
time: 457 us; the launch traced here: 448 us
  Pallas kernels  439 us (96%)
  local copies, waits for them, and re-layouts  9 us (2%)
    pallas_call x1, Pallas kernels, body(): pl.pallas_call(kernel, out_shape=jax.ShapeDtypeStruct(down_weight.shape,...  439 us

profile of v3, /device:TPU:120, one launch (start us, length us, event | category | flops | bytes accessed | tf_op | source)
XLA Modules:
  0.0 448.4 jit_solution(15477679360834403055)
XLA Ops:
  0.0 0.8 copy.6
  0.8 0.7 reshape.3.numer
  1.5 439.4 %gossip.1 = bf16[1,1792,2048]{2,1,0:T(8,128)(2,1)} custom-call(s32[192]{0:T(256)} %reshape.3.numer, bf16[256,2048]{1,0:T(8,128)(2,1)} %tokens.1, bf16[256,2048]{1,0:T(8,128)(2,1)} %targets.1, bf16[2048,1792]{1,0:T(8,128)(2,1)} %up.1, bf16[1,1792,2048]{2,1,0:T(8,128)(2,1)} %weight.1), custom_call_target="tpu_custom_call" | custom-call | tf_op jit(solution)/shard_map/gossip/pallas_call | solution.py:565
  440.9 7.5 %copy.8 = bf16[1,1792,2048]{2,1,0:T(8,128)(2,1)} copy(bf16[1,1792,2048]{2,1,0:T(8,128)(2,1)} %gossip.1) | data formatting | bytes 14680064

commit v4 on v3

--- a/solution.py
+++ b/solution.py
@@ -10,7 +10,9 @@
 MESH = pl.DeviceIdType.MESH
 LEARN_RATE = 2.0
 NW = 32
-WRAP_DEPTH = 2
+GRAD_ROWS = 896
+HEAD = 4
+WRAP_DEPTH = 3
 F32 = jnp.float32
 BF16 = jnp.bfloat16
 
@@ -22,7 +24,7 @@
 def kernel(numer, tokens, targets, up, weight, out,
            s, l1, r1, l2, r2, avg, rsx, piece, yrx, zrx, tok, hid, qrx, rrx, pown,
            ls, ts, tr, ps, pr, qs, qr, rs, rr,
-           gs, gr, xs, xr, as_, ar, ys, yr, zs, zr, os):
+           gs, gr, xs, xr, as_, ar, ys, yr, zs, zr, os, free):
     b, sh = lax.axis_index("blk"), lax.axis_index("shard")
     x, yh, z = b // 8, (b // 4) % 2, b % 4
     yl, e = sh // 2, sh % 2
@@ -51,6 +53,12 @@
     def send(src, dst, ss, rsem, dev):
         return pltpu.make_async_remote_copy(src, dst, ss, rsem, device_id=dev, device_id_type=MESH)
 
+    def when(cond, *fs):
+        @pl.when(cond)
+        def _():
+            for f in fs:
+                f()
+
     def up_a(j):
         return pltpu.make_async_copy(up.at[pl.ds(0, rows), pl.ds(j * width, width)], l2.at[j], ls.at[0, j])
 
@@ -68,7 +76,7 @@
         return p + core_at - 2 * p * core_at
 
     def spot(p, chip, core_from, core_at):
-        at_row = (which(p, core_at) * 2 + chip) * trow + core_from * tp
+        at_row = (chip * 2 + which(p, core_at)) * trow + core_from * tp
         return pl.ds(pl.multiple_of(at_row, tp), tp)
 
     def own_in(p):
@@ -120,16 +128,16 @@
     wr = jnp.where(z == 2, wr, 0.0)
     m = [[n(r, b, j) * 0.25 for j in range(3)] for r in range(2)]
 
-    def hidden(p, chip):
-        t = which(p, e) * 2 + chip
-        d = pl.ds(pl.multiple_of(t * trow, trow), trow)
+    def hidden(t, size):
+        d = pl.ds(pl.multiple_of(t * trow, trow), size * trow)
 
         def one(j, _):
             lanes = pl.ds(pl.multiple_of(j * width, width), width)
             a = dot(tok[d, :rows], l2[j]) + dot(tok[d, rows:], l2[slabs - 1, lanes, :])
-            h = a / (1.0 + jnp.exp(-a))
-            hid[d, lanes] = h.astype(BF16)
-            r2[t, lanes, :] = h.T.astype(BF16)
+            h = (a / (1.0 + jnp.exp(-a))).astype(BF16)
+            hid[d, lanes] = h
+            for k in range(size):
+                r2[t + k, lanes, :] = h[k * trow:(k + 1) * trow].T
             return 0
 
         lax.fori_loop(0, rows // width, one, 0)
@@ -143,11 +151,11 @@
         return pl.ds(pl.multiple_of(lo * trow + i, 64), trow if size is None else size)
 
     def c_p(c, chip):
-        return send(tok.at[block(2 + chip), lanes_of(c)], r2.at[4 + c // 3, block((c % 3) * 2 + chip)],
+        return send(tok.at[block(2 * chip + 1), lanes_of(c)], r2.at[4 + c // 3, block((c % 3) * 2 + chip)],
                     ps.at[c, chip], pr.at[c, chip], core)
 
     def c_q(c, chip):
-        return send(tok.at[block(chip), lanes_of(c)], qrx.at[c, block(chip)], qs.at[c, chip], qr.at[c, chip], mate)
+        return send(tok.at[block(2 * chip), lanes_of(c)], qrx.at[c, block(chip)], qs.at[c, chip], qr.at[c, chip], mate)
 
     def c_r(c):
         return send(qrx.at[c], rrx.at[c], rs.at[c], rr.at[c], core)
@@ -163,6 +171,10 @@
         return (lambda: send(src.at[c, d], dl.at[c, d], gs.at[0, i], gr.at[0, i], right),
                 lambda: send(src.at[c, d], dr.at[c, d], gs.at[1, i], gr.at[1, i], left))
 
+    def put(direction, those):
+        for i in those:
+            items(i)[direction]().start()
+
     def right_item(c, o, i):
         d = pl.ds(o * cr if isinstance(o, int) else pl.multiple_of(o * cr, cr), cr)
         return send(s.at[c, d], l1.at[c, d], gs.at[0, i], gr.at[0, i], right)
@@ -191,26 +203,17 @@
 
     def stage_a(c, chip):
         lanes = lanes_of(c)
-
-        def one(w, _):
-            rows_at = block(w * 2 + chip)
-            a = dot(hid[rows_at, :], s[c]) * scale
+        d = pl.ds(pl.multiple_of(chip * 2 * trow, 2 * trow), 2 * trow)
+        a = dot(hid[d, :], s[c]) * scale
+        for w in range(2):
             p = w + e - 2 * w * e
             y = piece[c, pl.ds(pl.multiple_of(p * tp, tp), tp), :].astype(F32)
             y = jnp.concatenate([y, y], axis=0)
-            a = a - jnp.where(jnp.logical_and(row_core == e, chip == yl), y, 0.0)
-
-            @pl.when(w == 0)
-            def _():
-                pown[...] = a
-
-            @pl.when(w == 1)
-            def _():
-                tok[rows_at, lanes] = a.astype(BF16)
-
-            return 0
-
-        lax.fori_loop(0, 2, one, 0)
+            aw = a[w * trow:(w + 1) * trow] - jnp.where(jnp.logical_and(row_core == e, chip == yl), y, 0.0)
+            if w == 0:
+                pown[...] = aw
+            else:
+                tok[block(chip * 2 + 1), lanes] = aw.astype(BF16)
         c_p(c, chip).start()
 
     def stage_b(c, chip):
@@ -220,11 +223,10 @@
         def one(i, _):
             other = r2[4 + c // 3, block((c % 3) * 2 + chip, i * 64, 64), :]
             mine = pown[pl.ds(pl.multiple_of(i * 64, 64), 64), :]
-            tok[block(chip, i * 64, 64), lanes] = (mine + other.astype(F32)).astype(BF16)
+            tok[block(2 * chip, i * 64, 64), lanes] = (mine + other.astype(F32)).astype(BF16)
             return 0
 
         lax.fori_loop(0, trow // 64, one, 0)
-        c_q(c, chip).start()
 
     def stage_c(c):
         for chip in range(2):
@@ -232,26 +234,28 @@
         lanes = lanes_of(c)
 
         def one(i, _):
-            o = pl.ds(pl.multiple_of(i * 64, 64), 64)
-            qrx[c, o, :] = (qrx[c, o, :].astype(F32) + tok[o, lanes].astype(F32)).astype(BF16)
+            for chip in range(2):
+                o = block(chip, i * 64, 64)
+                mine = tok[block(2 * chip, i * 64, 64), lanes]
+                qrx[c, o, :] = (qrx[c, o, :].astype(F32) + mine.astype(F32)).astype(BF16)
             return 0
 
-        lax.fori_loop(0, 2 * trow // 64, one, 0)
+        lax.fori_loop(0, trow // 64, one, 0)
         c_r(c).start()
 
     def stage_d(c):
         c_r(c).wait_recv()
 
         def one(i, _):
-            d = pl.ds(pl.multiple_of(i * width, width), width)
+            d = pl.ds(pl.multiple_of(i * GRAD_ROWS, GRAD_ROWS), GRAD_ROWS)
             g = dot(r2[0, d, :], qrx[c, :trow, :])
-            g += dot(r2[1, d, :], qrx[c, trow:, :])
-            g += dot(r2[2, d, :], rrx[c, :trow, :])
+            g += dot(r2[1, d, :], rrx[c, :trow, :])
+            g += dot(r2[2, d, :], qrx[c, trow:, :])
             g += dot(r2[3, d, :], rrx[c, trow:, :])
             s[c, d, :] = (s[c, d, :].astype(F32) - (LEARN_RATE * scale) * g).astype(BF16)
             return 0
 
-        lax.fori_loop(0, rows // width, one, 0)
+        lax.fori_loop(0, rows // GRAD_ROWS, one, 0)
         early(c)
 
     for p in range(2):
@@ -261,14 +265,15 @@
         up_b(j).wait()
     for p in range(2):
         t_core(p).wait_recv()
-        hidden(p, yl)
+    hidden(2 * yl, 2)
     for c in range(slabs):
         w_in(c).wait()
         t_in(c).wait()
 
     def own_step(i, _):
-        pl.when(i >= 1)(lambda: stage_b(i - 1, yl))
-        pl.when(i < slabs)(lambda: stage_a(i, yl))
+        when(i >= 1, lambda: stage_b(i - 1, yl))
+        when(jnp.logical_and(i >= 1, i <= HEAD), lambda: c_q(i - 1, yl).start())
+        when(i < slabs, lambda: stage_a(i, yl))
         return 0
 
     lax.fori_loop(0, slabs + 1, own_step, 0)
@@ -276,15 +281,19 @@
         t_mate(p).wait_recv()
         t_fwd(p).start()
         t_fwd(p).wait_recv()
-        hidden(p, 1 - yl)
+        hidden(2 * (1 - yl) + which(p, e), 1)
     for p in range(2):
         t_fwd(p).wait_send()
 
     def other_step(i, _):
-        pl.when(jnp.logical_and(i >= 1, i <= slabs))(lambda: stage_b(i - 1, 1 - yl))
-        pl.when(i >= 2)(lambda: stage_c(i - 2))
-        pl.when(i < slabs)(lambda: stage_a(i, 1 - yl))
-        pl.when(i >= 2)(lambda: stage_d(i - 2))
+        when(jnp.logical_and(i >= 1, i <= slabs), lambda: stage_b(i - 1, 1 - yl),
+             lambda: c_q(i - 1, 1 - yl).start())
+        when(jnp.logical_and(i >= 1, i <= slabs - HEAD), lambda: c_q(i - 1 + HEAD, yl).start())
+        when(jnp.logical_and(i == slabs, z == 3), lambda: put(0, range(WRAP_DEPTH)))
+        when(jnp.logical_and(i == slabs, z == 0), lambda: put(1, range(WRAP_DEPTH)))
+        when(i >= 2, lambda: stage_c(i - 2))
+        when(i < slabs, lambda: stage_a(i, 1 - yl))
+        when(i >= 2, lambda: stage_d(i - 2))
         return 0
 
     lax.fori_loop(0, slabs + 2, other_step, 0)
@@ -333,7 +342,7 @@
 
     def a_rs(g, j):
         xx = (x + j) % 4
-        return send(r1.at[own(g, xx, 0, quarter)], rsx.at[j - 1, pl.ds(g * per, per)],
+        return send(r1.at[own(g, xx, 0, quarter)], rsx.at[j - 1, pl.ds(g % 2 * per, per)],
                     xs.at[g, j - 1], xr.at[g, j - 1], at(xx, yh, z))
 
     def a_y(g):
@@ -348,7 +357,7 @@
         ref = avg.at[own(g, x, yh * half, half)]
         return send(ref, ref, ys.at[1, g], yr.at[1, g], ydev)
 
-    around = [g < groups - 1 for g in range(groups)]
+    around = [False] * groups
 
     def a_zb(g):
         to = at(x, yh, jnp.where(z == 1, 0, jnp.where(z == 2, 3, 3 - z)))
@@ -373,13 +382,10 @@
             ref, to = avg.at[own(g, (x + 1) % 4, half, half)], xm
         return send(ref, ref, as_.at[g, k], ar.at[g, k], to)
 
-    def when(cond, *fs):
-        @pl.when(cond)
-        def _():
-            for f in fs:
-                f()
 
     def e_rs(g):
+        if g >= 2:
+            pl.semaphore_wait(free.at[g - 2], 3)
         for j in (1, 2, 3):
             a_rs(g, j).start()
 
@@ -394,11 +400,14 @@
                 o = pl.ds(pl.multiple_of(x * quarter + i * 64, 64), 64)
                 t = r1[c, o, :].astype(F32)
                 for j in range(3):
-                    t += rsx[j, c, d, :].astype(F32)
+                    t += rsx[j, g % 2 * per + cc, d, :].astype(F32)
                 piece[c, d, :] = t.astype(BF16)
                 return 0
 
             lax.fori_loop(0, quarter // 64, one, 0)
+        if g < 2:
+            for j in (1, 2, 3):
+                pl.semaphore_signal(free.at[g], inc=1, device_id=at((x + j) % 4, yh, z), device_id_type=MESH)
         a_y(g).start()
 
     def add_half(g, other, final):
@@ -472,8 +481,8 @@
                (7, 9, 10, 14, 15, 16, 18, 20),
                (11, 13, 14, 18, 19, 20, 22, 24),
                (15, 17, 18, 22, 23, 24, 26, 28))
-    plan_out = ((11, 13, 15, 17), (15, 17, 19, 21), (19, 21, 23, 25), (None, 24, 26, 28))
-    plan_way = ((11, 13, 15, 17, 19), (15, 17, 19, 21, 23), (19, 21, 23, 25, 27), (None, 24, 26, 28, 30))
+    plan_out = ((None, 12, 14, 16), (None, 16, 18, 20), (None, 20, 22, 24), (None, 24, 26, 28))
+    plan_way = ((None, 12, 14, 16, 18), (None, 16, 18, 20, 22), (None, 20, 22, 24, 26), (None, 24, 26, 28, 30))
     ways = [functools.partial(e_w, k) for k in range(3)]
     inside, outside, special = {}, {}, {}
     for g in range(groups):
@@ -493,10 +502,6 @@
     for i in range(chunks, 2 * chunks):
         bulk.setdefault(max(i - chunks, slabs), []).append(i)
 
-    def put(direction, those):
-        for i in those:
-            items(i)[direction]().start()
-
     def issue(slot):
         if slot in jit:
             when(inner, lambda: put(0, jit[slot]), lambda: put(1, jit[slot]))
@@ -504,8 +509,6 @@
             when(z == 3, lambda: put(0, wrap.get(slot, ())), lambda: put(1, bulk.get(slot, ())))
             when(z == 0, lambda: put(1, wrap.get(slot, ())), lambda: put(0, bulk.get(slot, ())))
 
-    when(z == 3, lambda: put(0, range(WRAP_DEPTH)))
-    when(z == 0, lambda: put(1, range(WRAP_DEPTH)))
     ready = []
     for slot in range(2 * chunks):
         for cp in items(slot):
@@ -554,6 +557,40 @@
         o_copy(i).wait()
 
 
+def copy_kernel(src, dst, held, isem, osem):
+    parts = held.shape[0]
+    size = src.shape[1] // parts
+
+    def move(i, back):
+        there = pl.ds(i * size, size)
+        if back:
+            return pltpu.make_async_copy(held.at[i], dst.at[0, there], osem.at[i])
+        return pltpu.make_async_copy(src.at[0, there], held.at[i], isem.at[i])
+
+    for i in range(parts):
+        move(i, False).start()
+    for i in range(parts):
+        move(i, False).wait()
+        move(i, True).start()
+    for i in range(parts):
+        move(i, True).wait()
+
+
+def copy_call(a):
+    parts = 14
+    any_ = pl.BlockSpec(memory_space=pl.ANY)
+    return pl.pallas_call(
+        copy_kernel,
+        out_shape=jax.ShapeDtypeStruct(a.shape, a.dtype),
+        in_specs=[any_],
+        out_specs=any_,
+        scratch_shapes=[pltpu.VMEM((parts, a.shape[1] // parts, a.shape[2]), a.dtype),
+                        pltpu.SemaphoreType.DMA((parts,)), pltpu.SemaphoreType.DMA((parts,))],
+        compiler_params=pltpu.CompilerParams(vmem_limit_bytes=67_043_328),
+        name="place",
+    )(a)
+
+
 def body(tokens, targets, up_weight, down_weight, mix_numer):
     rows, dim = down_weight.shape[1:]
     slabs = 8
@@ -562,13 +599,13 @@
     D = pltpu.SemaphoreType.DMA
     vm = lambda *shape: pltpu.VMEM(shape, BF16)
     any_ = pl.BlockSpec(memory_space=pl.ANY)
-    return pl.pallas_call(
+    return copy_call(pl.pallas_call(
         kernel,
         out_shape=jax.ShapeDtypeStruct(down_weight.shape, BF16),
         in_specs=[pl.BlockSpec(memory_space=pltpu.SMEM)] + [any_] * 4,
         out_specs=any_,
         scratch_shapes=[vm(slabs, rows, width)] * 6 + [
-            vm(3, slabs, rows // 4, width), vm(slabs, rows // 4, width),
+            vm(3, slabs // 2, rows // 4, width), vm(slabs, rows // 4, width),
             vm(slabs, rows // 8, width), vm(slabs, rows // 8, width),
             vm(4 * trow, dim), vm(4 * trow, rows),
             vm(slabs, 2 * trow, width), vm(slabs, 2 * trow, width),
@@ -576,12 +613,12 @@
             D((5, slabs)), D((3, 2)), D((3, 2)),
             D((slabs, 2)), D((slabs, 2)), D((slabs, 2)), D((slabs, 2)), D((slabs,)), D((slabs,)),
             D((2, 4 * slabs)), D((2, 4 * slabs)), D((4, 3)), D((4, 3)), D((4, 4)), D((4, 4)),
-            D((2, 4)), D((2, 4)), D((3, 4)), D((3, 4)), D((4 * slabs,)),
+            D((2, 4)), D((2, 4)), D((3, 4)), D((3, 4)), D((4 * slabs,)), pltpu.SemaphoreType.REGULAR((2,)),
         ],
         compiler_params=pltpu.CompilerParams(
             collective_id=0, has_side_effects=True, vmem_limit_bytes=67_043_328),
         name="gossip",
-    )(mix_numer.reshape(-1), tokens, targets, up_weight, down_weight)
+    )(mix_numer.reshape(-1), tokens, targets, up_weight, down_weight))
 
 
 def solution(mesh):

time: 457 us -> 418 us (0.915)
  Pallas kernels: 439 us -> 412 us
  local copies, waits for them, and re-layouts: 9 us -> 1.47 us
    pallas_call x1, Pallas kernels: 439 us -> 406 us  [body(): pl.pallas_call(kernel, out_shape=jax.ShapeDtypeStruct(down_weight.shape,...]
    unnamed x2 -> x1, local copies, waits for them, and re-layouts: 8.3 us -> 0.77 us
    pallas_call x0 -> x1, Pallas kernels: none -> 5.97 us  [copy_call(): pl.pallas_call(copy_kernel, out_shape=jax.ShapeDtypeStruct(a.shape, a.dty...]
where the time goes in v4:
time: 418 us; the launch traced here: 414 us
  Pallas kernels  412 us (99%)
    pallas_call x1, Pallas kernels, body(): pl.pallas_call(kernel, out_shape=jax.ShapeDtypeStruct(down_weight.shape,...  406 us

profile of v4, /device:TPU:120, one launch (start us, length us, event | category | flops | bytes accessed | tf_op | source)
XLA Modules:
  0.0 413.9 jit_solution(5744051304585143635)
XLA Ops:
  0.0 0.8 copy.6
  0.8 0.7 reshape.3.numer
  1.5 406.5 %gossip.1.src = bf16[1,1792,2048]{2,1,0:T(8,128)(2,1)} custom-call(s32[192]{0:T(256)} %reshape.3.numer, bf16[256,2048]{1,0:T(8,128)(2,1)} %tokens.1, bf16[256,2048]{1,0:T(8,128)(2,1)} %targets.1, bf16[2048,1792]{1,0:T(8,128)(2,1)} %up.1, bf16[1,1792,2048]{2,1,0:T(8,128)(2,1)} %weight.1), custom_call_target="tpu_custom_call" | custom-call | tf_op jit(solution)/shard_map/gossip/pallas_call | solution.py:602
  408.0 6.0 %place.1 = bf16[1,1792,2048]{2,1,0:T(8,128)(2,1)} custom-call(bf16[1,1792,2048]{2,1,0:T(8,128)(2,1)} %gossip.1.src), custom_call_target="tpu_custom_call" | custom-call | tf_op jit(solution)/shard_map/place/pallas_call | solution.py:582

commit v5 on v4

--- a/solution.py
+++ b/solution.py
@@ -12,6 +12,9 @@
 NW = 32
 GRAD_ROWS = 896
 HEAD = 4
+RELAY_AT = 3
+RING = 4
+LAGS = (0, 2, 3, 6, 7, 8, 9)
 WRAP_DEPTH = 3
 F32 = jnp.float32
 BF16 = jnp.bfloat16
@@ -22,7 +25,7 @@
 
 
 def kernel(numer, tokens, targets, up, weight, out,
-           s, l1, r1, l2, r2, avg, rsx, piece, yrx, zrx, tok, hid, qrx, rrx, pown,
+           s, l1, r1, l2, r2, avg, rsx, piece, yrx, zrx, tok, hid, qrx, rrx, pown, rel, rels, relr,
            ls, ts, tr, ps, pr, qs, qr, rs, rr,
            gs, gr, xs, xr, as_, ar, ys, yr, zs, zr, os, free):
     b, sh = lax.axis_index("blk"), lax.axis_index("shard")
@@ -31,7 +34,7 @@
     slabs, rows, width = s.shape
     chunks, cr = 2 * slabs, rows // 2
     ff, dim = 4 * rows, slabs * width
-    groups, per = 4, slabs // 4
+    groups = slabs
     quarter, half = rows // 4, rows // 8
     trow = tokens.shape[0]
     tp = trow // 2
@@ -45,10 +48,8 @@
     zdev = at(x, yh, 3 - z)
     xp, xm = at((x + 1) % 4, yh, z), at((x + 3) % 4, yh, z)
     inner = jnp.logical_or(z == 1, z == 2)
-    outer = jnp.logical_or(z == 0, z == 3)
-    loaded = jnp.logical_or(jnp.logical_and(z == 0, yh == 0), jnp.logical_and(z == 3, yh == 1))
-    plain = jnp.logical_and(outer, jnp.logical_not(loaded))
-    way = jnp.where(z == 0, 1, 3)
+    outer = jnp.logical_not(inner)
+    beside = (b + jnp.where(z % 2 == 0, 1, 31)) % 32
 
     def send(src, dst, ss, rsem, dev):
         return pltpu.make_async_remote_copy(src, dst, ss, rsem, device_id=dev, device_id_type=MESH)
@@ -98,10 +99,15 @@
         up_b(j).start()
 
     barrier = pltpu.get_barrier_semaphore()
-    for dev in (core, mate, left, right, xp, at((x + 2) % 4, yh, z), xm,
-                ydev, at(x, yh, (z + 1) % 4), at(x, yh, (z + 3) % 4)):
+    for dev in (core, mate, left, right, (beside, mate[1])):
         pl.semaphore_signal(barrier, inc=1, device_id=dev, device_id_type=MESH)
-    pl.semaphore_wait(barrier, 10)
+
+    @pl.when(inner)
+    def _():
+        for dev in (xp, at((x + 2) % 4, yh, z), xm, ydev):
+            pl.semaphore_signal(barrier, inc=1, device_id=dev, device_id_type=MESH)
+
+    pl.semaphore_wait(barrier, jnp.where(inner, 9, 5))
 
     for p in range(2):
         t_mate(p).start()
@@ -157,6 +163,13 @@
     def c_q(c, chip):
         return send(tok.at[block(2 * chip), lanes_of(c)], qrx.at[c, block(chip)], qs.at[c, chip], qr.at[c, chip], mate)
 
+    def relay_out(c):
+        return send(tok.at[block(2 * yl), lanes_of(c)], rel.at[c - HEAD], qs.at[c, yl], relr.at[c - HEAD],
+                    (beside, sh))
+
+    def relay_on(k):
+        return send(rel.at[k], qrx.at[HEAD + k, block(yl)], rels.at[k], qr.at[HEAD + k, yl], (beside, mate[1]))
+
     def c_r(c):
         return send(qrx.at[c], rrx.at[c], rs.at[c], rr.at[c], core)
 
@@ -165,15 +178,15 @@
         d = pl.ds(o * cr, cr)
         return c, d
 
-    def items(i):
+    def items(i, later=None):
         c, d = item(i)
-        src, dl, dr = (s, l1, r1) if i < chunks else (l1, l2, r2)
+        src, dl, dr = (s, l1, r1) if i < chunks else (l1 if later is None else later, l2, r2)
         return (lambda: send(src.at[c, d], dl.at[c, d], gs.at[0, i], gr.at[0, i], right),
                 lambda: send(src.at[c, d], dr.at[c, d], gs.at[1, i], gr.at[1, i], left))
 
-    def put(direction, those):
+    def put(direction, those, later=None):
         for i in those:
-            items(i)[direction]().start()
+            items(i, later)[direction]().start()
 
     def right_item(c, o, i):
         d = pl.ds(o * cr if isinstance(o, int) else pl.multiple_of(o * cr, cr), cr)
@@ -273,6 +286,7 @@
     def own_step(i, _):
         when(i >= 1, lambda: stage_b(i - 1, yl))
         when(jnp.logical_and(i >= 1, i <= HEAD), lambda: c_q(i - 1, yl).start())
+        when(jnp.logical_and(i > HEAD, outer), lambda: relay_out(i - 1).start())
         when(i < slabs, lambda: stage_a(i, yl))
         return 0
 
@@ -288,7 +302,15 @@
     def other_step(i, _):
         when(jnp.logical_and(i >= 1, i <= slabs), lambda: stage_b(i - 1, 1 - yl),
              lambda: c_q(i - 1, 1 - yl).start())
-        when(jnp.logical_and(i >= 1, i <= slabs - HEAD), lambda: c_q(i - 1 + HEAD, yl).start())
+
+        @pl.when(jnp.logical_and(i == RELAY_AT, inner))
+        def _():
+            for k in range(slabs - HEAD):
+                relay_out(HEAD + k).wait_recv()
+                relay_on(k).start()
+
+        when(jnp.logical_and(jnp.logical_and(i >= 1, i <= slabs - HEAD), inner),
+             lambda: c_q(i - 1 + HEAD, yl).start())
         when(jnp.logical_and(i == slabs, z == 3), lambda: put(0, range(WRAP_DEPTH)))
         when(jnp.logical_and(i == slabs, z == 0), lambda: put(1, range(WRAP_DEPTH)))
         when(i >= 2, lambda: stage_c(i - 2))
@@ -319,57 +341,59 @@
             r1[c, d, :] = (wb * a + wl * p + wr * q).astype(BF16)
         over(i, body)
 
-    def second(i):
-        def body(c, d):
-            a = l1[c, d, :].astype(F32)
-            p = l2[c, d, :].astype(F32)
-            q = r2[c, d, :].astype(F32)
-            l2[c, d, :] = (m[1][0] * a + m[1][1] * p + m[1][2] * q).astype(BF16)
-        over(i, body)
+    def mixed(c, d):
+        a = l1[c, d, :].astype(F32)
+        p = l2[c, d, :].astype(F32)
+        q = r2[c, d, :].astype(F32)
+        return m[1][0] * a + m[1][1] * p + m[1][2] * q
 
     def o_copy(i):
         c, d = item(i)
         return pltpu.make_async_copy(l2.at[c, d], out.at[0, d, pl.ds(c * width, width)], os.at[i])
 
-    def last(i):
+    def second(i):
+        def inside(c, d):
+            l2[c, d, :] = (mixed(c, d) - avg[c, d, :].astype(F32)).astype(BF16)
+
+        def outside(c, d):
+            l2[c, d, :] = mixed(c, d).astype(BF16)
+
+        when(inner, lambda: over(i, inside))
+        when(jnp.logical_not(inner), lambda: over(i, outside))
+        o_copy(i).start()
+
+    unmix = 4.0 / jnp.where(z == 1, n(1, kl, 2), n(1, kr, 1))
+
+    def outward(i):
+        g = (i % chunks) // 2
+        if i % 2 == 0:
+            for j in (1, 2, 3):
+                a_rs(g, j).wait_send()
+
         def body(c, d):
-            l2[c, d, :] = (l2[c, d, :].astype(F32) - avg[c, d, :].astype(F32)).astype(BF16)
+            r1[c, d, :] = (l1[c, d, :].astype(F32) - unmix * avg[c, d, :].astype(F32)).astype(BF16)
+
         over(i, body)
-        o_copy(i).start()
 
     def own(g, xx, lo, size):
-        return (pl.ds(g * per, per), pl.ds(pl.multiple_of(xx * quarter + lo, 32), size), slice(None))
+        return (g, pl.ds(pl.multiple_of(xx * quarter + lo, 32), size))
 
     def a_rs(g, j):
         xx = (x + j) % 4
-        return send(r1.at[own(g, xx, 0, quarter)], rsx.at[j - 1, pl.ds(g % 2 * per, per)],
+        return send(r1.at[own(g, xx, 0, quarter)], rsx.at[j - 1, g % RING],
                     xs.at[g, j - 1], xr.at[g, j - 1], at(xx, yh, z))
 
     def a_y(g):
-        return send(piece.at[pl.ds(g * per, per), pl.ds(pl.multiple_of((1 - yh) * half, 32), half)],
-                    yrx.at[pl.ds(g * per, per)], ys.at[0, g], yr.at[0, g], ydev)
+        return send(piece.at[g, pl.ds(pl.multiple_of((1 - yh) * half, 32), half)],
+                    yrx.at[g], ys.at[0, g], yr.at[0, g], ydev)
 
     def a_z(g):
-        return send(piece.at[pl.ds(g * per, per), pl.ds(pl.multiple_of(yh * half, 32), half)],
-                    zrx.at[pl.ds(g * per, per)], zs.at[0, g], zr.at[0, g], zdev)
+        return send(piece.at[g, pl.ds(pl.multiple_of(yh * half, 32), half)],
+                    zrx.at[g], zs.at[g], zr.at[g], zdev)
 
     def a_yg(g):
         ref = avg.at[own(g, x, yh * half, half)]
         return send(ref, ref, ys.at[1, g], yr.at[1, g], ydev)
-
-    around = [False] * groups
-
-    def a_zb(g):
-        to = at(x, yh, jnp.where(z == 1, 0, jnp.where(z == 2, 3, 3 - z)))
-        if around[g]:
-            ref = avg.at[own(g, x, jnp.where(z <= 1, 0, half), half)]
-        else:
-            ref = avg.at[own(g, x, 0, quarter)]
-        return send(ref, ref, zs.at[1, g], zr.at[1, g], to)
-
-    def a_zf(g):
-        ref = avg.at[own(g, x, jnp.where(z <= 1, 0, half), half)]
-        return send(ref, ref, zs.at[2, g], zr.at[2, g], zdev)
 
     def a_x(g, k):
         if k == 0:
@@ -384,48 +408,42 @@
 
 
     def e_rs(g):
-        if g >= 2:
-            pl.semaphore_wait(free.at[g - 2], 3)
+        if g >= RING:
+            pl.semaphore_wait(free.at[g - RING], 3)
         for j in (1, 2, 3):
             a_rs(g, j).start()
 
     def e_y(g):
         for j in (1, 2, 3):
             a_rs(g, j).wait_recv()
-        for cc in range(per):
-            c = g * per + cc
-
-            def one(i, _):
-                d = pl.ds(pl.multiple_of(i * 64, 64), 64)
-                o = pl.ds(pl.multiple_of(x * quarter + i * 64, 64), 64)
-                t = r1[c, o, :].astype(F32)
-                for j in range(3):
-                    t += rsx[j, g % 2 * per + cc, d, :].astype(F32)
-                piece[c, d, :] = t.astype(BF16)
-                return 0
-
-            lax.fori_loop(0, quarter // 64, one, 0)
-        if g < 2:
+        def one(i, _):
+            d = pl.ds(pl.multiple_of(i * 64, 64), 64)
+            o = pl.ds(pl.multiple_of(x * quarter + i * 64, 64), 64)
+            t = r1[g, o, :].astype(F32)
+            for j in range(3):
+                t += rsx[j, g % RING, d, :].astype(F32)
+            piece[g, d, :] = t.astype(BF16)
+            return 0
+
+        lax.fori_loop(0, quarter // 64, one, 0)
+        if g < groups - RING:
             for j in (1, 2, 3):
                 pl.semaphore_signal(free.at[g], inc=1, device_id=at((x + j) % 4, yh, z), device_id_type=MESH)
         a_y(g).start()
 
     def add_half(g, other, final):
-        for cc in range(per):
-            c = g * per + cc
-
-            def one(i, _):
-                d = pl.ds(pl.multiple_of(i * 32, 32), 32)
-                o = pl.ds(pl.multiple_of(yh * half + i * 32, 32), 32)
-                t = piece[c, o, :].astype(F32) + other[c, d, :].astype(F32)
-                if final:
-                    p = pl.ds(pl.multiple_of(x * quarter + yh * half + i * 32, 32), 32)
-                    avg[c, p, :] = (t * (1.0 / NW)).astype(BF16)
-                else:
-                    piece[c, o, :] = t.astype(BF16)
-                return 0
-
-            lax.fori_loop(0, half // 32, one, 0)
+        def one(i, _):
+            d = pl.ds(pl.multiple_of(i * 32, 32), 32)
+            o = pl.ds(pl.multiple_of(yh * half + i * 32, 32), 32)
+            t = piece[g, o, :].astype(F32) + other[g, d, :].astype(F32)
+            if final:
+                p = pl.ds(pl.multiple_of(x * quarter + yh * half + i * 32, 32), 32)
+                avg[g, p, :] = (t * (1.0 / NW)).astype(BF16)
+            else:
+                piece[g, o, :] = t.astype(BF16)
+            return 0
+
+        lax.fori_loop(0, half // 32, one, 0)
 
     def e_z(g):
         a_y(g).wait_recv()
@@ -437,21 +455,10 @@
         add_half(g, zrx, True)
         a_yg(g).start()
 
-    def e_zb(g):
+    def e_x0(g):
         a_yg(g).wait_recv()
-        a_zb(g).start()
-
-    def e_zf(g):
-        a_zb(g).wait_recv()
-        a_zf(g).start()
-
-    def e_x0(g):
         a_x(g, 0).start()
         a_x(g, 1).start()
-
-    def e_x0_out(g):
-        (a_zf if around[g] else a_zb)(g).wait_recv()
-        e_x0(g)
 
     def e_x1(g):
         a_x(g, 0).wait_recv()
@@ -463,37 +470,10 @@
         a_x(g, 2).wait_recv()
         a_x(g, 3).wait_recv()
 
-    def a_way(g, k):
-        ref = avg.at[own(g, (x + k * (4 - way)) % 4, 0, quarter)]
-        return send(ref, ref, as_.at[g, k], ar.at[g, k], at((x + way) % 4, yh, z))
-
-    def e_w0(g):
-        (a_zf if around[g] else a_zb)(g).wait_recv()
-        a_way(g, 0).start()
-
-    def e_w(k, g):
-        a_way(g, k).wait_recv()
-        if k < 2:
-            a_way(g, k + 1).start()
-
-    stages = (e_rs, e_y, e_z, e_yg, e_zb, e_x0, e_x1, e_x2)
-    plan_in = ((3, 5, 6, 10, 11, 12, 14, 16),
-               (7, 9, 10, 14, 15, 16, 18, 20),
-               (11, 13, 14, 18, 19, 20, 22, 24),
-               (15, 17, 18, 22, 23, 24, 26, 28))
-    plan_out = ((None, 12, 14, 16), (None, 16, 18, 20), (None, 20, 22, 24), (None, 24, 26, 28))
-    plan_way = ((None, 12, 14, 16, 18), (None, 16, 18, 20, 22), (None, 20, 22, 24, 26), (None, 24, 26, 28, 30))
-    ways = [functools.partial(e_w, k) for k in range(3)]
-    inside, outside, special = {}, {}, {}
+    inside = {}
     for g in range(groups):
-        for f, slot in zip(stages, plan_in[g]):
-            inside.setdefault(slot, []).append((f, g))
-        for f, slot in zip((e_zf, e_x0_out, e_x1, e_x2), plan_out[g]):
-            if slot is not None:
-                outside.setdefault(slot, []).append((f, g))
-        for f, slot in zip((e_zf, e_w0, *ways), plan_way[g]):
-            if slot is not None:
-                special.setdefault(slot, []).append((f, g))
+        for f, lag in zip((e_rs, e_y, e_z, e_yg, e_x0, e_x1, e_x2), LAGS):
+            inside.setdefault(2 * g + 1 + lag, []).append(functools.partial(f, g))
     jit, wrap, bulk = {}, {}, {}
     for i in range(slabs, 2 * chunks):
         jit.setdefault(i - 3 if i < chunks else max(i - 3, chunks - 2), []).append(i)
@@ -504,12 +484,16 @@
 
     def issue(slot):
         if slot in jit:
-            when(inner, lambda: put(0, jit[slot]), lambda: put(1, jit[slot]))
-        if slot in wrap or slot in bulk:
-            when(z == 3, lambda: put(0, wrap.get(slot, ())), lambda: put(1, bulk.get(slot, ())))
-            when(z == 0, lambda: put(1, wrap.get(slot, ())), lambda: put(0, bulk.get(slot, ())))
-
-    ready = []
+            @pl.when(inner)
+            def _():
+                for i in jit[slot]:
+                    if i >= chunks:
+                        outward(i)
+            when(z == 1, lambda: put(0, jit[slot]), lambda: put(1, jit[slot], r1))
+            when(z == 2, lambda: put(1, jit[slot]), lambda: put(0, jit[slot], r1))
+        when(z == 3, lambda: put(0, wrap.get(slot, ())), lambda: put(1, bulk.get(slot, ())))
+        when(z == 0, lambda: put(1, wrap.get(slot, ())), lambda: put(0, bulk.get(slot, ())))
+
     for slot in range(2 * chunks):
         for cp in items(slot):
             cp().wait_recv()
@@ -517,19 +501,9 @@
             first(slot)
         else:
             second(slot)
+        if slot in inside:
+            when(inner, *inside[slot])
         issue(slot)
-        if slot in inside:
-            when(inner, *[functools.partial(f, g) for f, g in inside[slot]])
-        if slot in outside:
-            when(plain, *[functools.partial(f, g) for f, g in outside[slot]])
-        if slot in special:
-            when(loaded, *[functools.partial(f, g) for f, g in special[slot]])
-        if slot >= chunks:
-            ready.append(slot)
-            for i in [i for i in ready if max(p[(i - chunks) // (2 * per)][-1] for p in (plan_in, plan_out, plan_way)) <= slot]:
-                last(i)
-                ready.remove(i)
-    assert not ready
 
     for p in range(2):
         t_core(p).wait_send()
@@ -542,17 +516,17 @@
     for i in range(2 * chunks):
         for cp in items(i):
             cp().wait_send()
-    for g in range(groups):
-        def drain():
-            for j in (1, 2, 3):
-                a_rs(g, j).wait_send()
-            for f in (a_y, a_z, a_yg, a_zb):
+
+    @pl.when(inner)
+    def _():
+        for g in range(groups):
+            for f in (a_y, a_z, a_yg):
                 f(g).wait_send()
-        when(inner, drain)
-        if around[g]:
-            when(outer, lambda: a_zf(g).wait_send())
-        when(loaded, *[a_way(g, k).wait_send for k in range(3)])
-        when(jnp.logical_not(loaded), *[a_x(g, k).wait_send for k in range(4)])
+            if g < slabs - HEAD:
+                relay_on(g).wait_send()
+            for k in range(4):
+                a_x(g, k).wait_send()
+
     for i in range(chunks, 2 * chunks):
         o_copy(i).wait()
 
@@ -605,15 +579,16 @@
         in_specs=[pl.BlockSpec(memory_space=pltpu.SMEM)] + [any_] * 4,
         out_specs=any_,
         scratch_shapes=[vm(slabs, rows, width)] * 6 + [
-            vm(3, slabs // 2, rows // 4, width), vm(slabs, rows // 4, width),
+            vm(3, RING, rows // 4, width), vm(slabs, rows // 4, width),
             vm(slabs, rows // 8, width), vm(slabs, rows // 8, width),
             vm(4 * trow, dim), vm(4 * trow, rows),
             vm(slabs, 2 * trow, width), vm(slabs, 2 * trow, width),
-            pltpu.VMEM((trow, width), F32),
+            pltpu.VMEM((trow, width), F32), vm(slabs - HEAD, trow, width), D((slabs - HEAD,)), D((slabs - HEAD,)),
             D((5, slabs)), D((3, 2)), D((3, 2)),
             D((slabs, 2)), D((slabs, 2)), D((slabs, 2)), D((slabs, 2)), D((slabs,)), D((slabs,)),
-            D((2, 4 * slabs)), D((2, 4 * slabs)), D((4, 3)), D((4, 3)), D((4, 4)), D((4, 4)),
-            D((2, 4)), D((2, 4)), D((3, 4)), D((3, 4)), D((4 * slabs,)), pltpu.SemaphoreType.REGULAR((2,)),
+            D((2, 4 * slabs)), D((2, 4 * slabs)), D((slabs, 3)), D((slabs, 3)), D((slabs, 4)), D((slabs, 4)),
+            D((2, slabs)), D((2, slabs)), D((slabs,)), D((slabs,)), D((4 * slabs,)),
+            pltpu.SemaphoreType.REGULAR((slabs - RING,)),
         ],
         compiler_params=pltpu.CompilerParams(
             collective_id=0, has_side_effects=True, vmem_limit_bytes=67_043_328),

time: 418 us -> 410 us (0.981)
  Pallas kernels: 412 us -> 403 us
    pallas_call x1, Pallas kernels: 406 us -> 397 us  [body(): pl.pallas_call(kernel, out_shape=jax.ShapeDtypeStruct(down_weight.shape,...]
where the time goes in v5:
time: 410 us; the launch traced here: 404 us
  Pallas kernels  403 us (98%)
    pallas_call x1, Pallas kernels, body(): pl.pallas_call(kernel, out_shape=jax.ShapeDtypeStruct(down_weight.shape,...  397 us

profile of v5, /device:TPU:120, one launch (start us, length us, event | category | flops | bytes accessed | tf_op | source)
XLA Modules:
  0.0 404.3 jit_solution(16565565629233633556)
XLA Ops:
  0.0 0.8 copy.6
  0.8 0.7 reshape.3.numer
  1.5 396.9 %gossip.1.src = bf16[1,1792,2048]{2,1,0:T(8,128)(2,1)} custom-call(s32[192]{0:T(256)} %reshape.3.numer, bf16[256,2048]{1,0:T(8,128)(2,1)} %tokens.1, bf16[256,2048]{1,0:T(8,128)(2,1)} %targets.1, bf16[2048,1792]{1,0:T(8,128)(2,1)} %up.1, bf16[1,1792,2048]{2,1,0:T(8,128)(2,1)} %weight.1), custom_call_target="tpu_custom_call" | custom-call | tf_op jit(solution)/shard_map/gossip/pallas_call | solution.py:576
  398.3 6.0 %place.1 = bf16[1,1792,2048]{2,1,0:T(8,128)(2,1)} custom-call(bf16[1,1792,2048]{2,1,0:T(8,128)(2,1)} %gossip.1.src), custom_call_target="tpu_custom_call" | custom-call | tf_op jit(solution)/shard_map/place/pallas_call | solution.py:556

commit v6 on v5

--- a/solution.py
+++ b/solution.py
@@ -13,6 +13,9 @@
 GRAD_ROWS = 896
 HEAD = 4
 RELAY_AT = 3
+LAG = (2, 4)
+HEAD_IN = 4
+PAIR = 2
 RING = 4
 LAGS = (0, 2, 3, 6, 7, 8, 9)
 WRAP_DEPTH = 3
@@ -92,21 +95,21 @@
     def t_fwd(p):
         return send(tok.at[spot(p, 1 - yl, e, e)], tok.at[spot(p, 1 - yl, e, 1 - e)], ts.at[2, p], tr.at[2, p], core)
 
+    barrier = pltpu.get_barrier_semaphore()
+    for dev in (core, mate, left, right, (beside, mate[1])):
+        pl.semaphore_signal(barrier, inc=1, device_id=dev, device_id_type=MESH)
+
+    @pl.when(inner)
+    def _():
+        for dev in (xp, at((x + 2) % 4, yh, z), xm, ydev):
+            pl.semaphore_signal(barrier, inc=1, device_id=dev, device_id_type=MESH)
+
     for p in range(2):
         own_in(p).start()
     for j in range(rows // width):
         up_a(j).start()
         up_b(j).start()
 
-    barrier = pltpu.get_barrier_semaphore()
-    for dev in (core, mate, left, right, (beside, mate[1])):
-        pl.semaphore_signal(barrier, inc=1, device_id=dev, device_id_type=MESH)
-
-    @pl.when(inner)
-    def _():
-        for dev in (xp, at((x + 2) % 4, yh, z), xm, ydev):
-            pl.semaphore_signal(barrier, inc=1, device_id=dev, device_id_type=MESH)
-
     pl.semaphore_wait(barrier, jnp.where(inner, 9, 5))
 
     for p in range(2):
@@ -118,7 +121,7 @@
         t_in(c).start()
 
     def n(r, k, j):
-        return numer[r * 96 + k * 3 + j].astype(F32)
+        return numer[r, k, j].astype(F32)
 
     kl, kr, kll, krr = (b + 31) % 32, (b + 1) % 32, (b + 30) % 32, (b + 2) % 32
 
@@ -137,16 +140,29 @@
     def hidden(t, size):
         d = pl.ds(pl.multiple_of(t * trow, trow), size * trow)
 
+        def tiles(j, many):
+            at_j = [j + k for k in range(many)]
+            lanes = [pl.ds(pl.multiple_of(jj * width, width), width) for jj in at_j]
+            above = jnp.concatenate([l2[jj] for jj in at_j], axis=1)
+            below = jnp.concatenate([l2[slabs - 1, n, :] for n in lanes], axis=1)
+            a = dot(tok[d, :rows], above) + dot(tok[d, rows:], below)
+            h = (a / (1.0 + jnp.exp(-a))).astype(BF16)
+            for i, n in enumerate(lanes):
+                hh = h[:, i * width:(i + 1) * width]
+                hid[d, n] = hh
+                for k in range(size):
+                    r2[t + k, n, :] = hh[k * trow:(k + 1) * trow].T
+
+        many = PAIR if size == 1 else 1
+        whole = rows // width // many
+
         def one(j, _):
-            lanes = pl.ds(pl.multiple_of(j * width, width), width)
-            a = dot(tok[d, :rows], l2[j]) + dot(tok[d, rows:], l2[slabs - 1, lanes, :])
-            h = (a / (1.0 + jnp.exp(-a))).astype(BF16)
-            hid[d, lanes] = h
-            for k in range(size):
-                r2[t + k, lanes, :] = h[k * trow:(k + 1) * trow].T
+            tiles(j * many, many)
             return 0
 
-        lax.fori_loop(0, rows // width, one, 0)
+        lax.fori_loop(0, whole, one, 0)
+        for j in range(whole * many, rows // width):
+            tiles(j, 1)
 
     scale = ff ** -0.5
 
@@ -285,7 +301,7 @@
 
     def own_step(i, _):
         when(i >= 1, lambda: stage_b(i - 1, yl))
-        when(jnp.logical_and(i >= 1, i <= HEAD), lambda: c_q(i - 1, yl).start())
+        when(jnp.logical_and(i >= 1, i <= jnp.where(inner, HEAD_IN, HEAD)), lambda: c_q(i - 1, yl).start())
         when(jnp.logical_and(i > HEAD, outer), lambda: relay_out(i - 1).start())
         when(i < slabs, lambda: stage_a(i, yl))
         return 0
@@ -309,16 +325,18 @@
                 relay_out(HEAD + k).wait_recv()
                 relay_on(k).start()
 
-        when(jnp.logical_and(jnp.logical_and(i >= 1, i <= slabs - HEAD), inner),
-             lambda: c_q(i - 1 + HEAD, yl).start())
+        when(jnp.logical_and(jnp.logical_and(i >= 1, i <= slabs - HEAD_IN), inner),
+             lambda: c_q(i - 1 + HEAD_IN, yl).start())
         when(jnp.logical_and(i == slabs, z == 3), lambda: put(0, range(WRAP_DEPTH)))
         when(jnp.logical_and(i == slabs, z == 0), lambda: put(1, range(WRAP_DEPTH)))
-        when(i >= 2, lambda: stage_c(i - 2))
+        behind = i - jnp.where(inner, LAG[0], LAG[1])
+        due = jnp.logical_and(behind >= 0, behind < slabs)
+        when(due, lambda: stage_c(behind))
         when(i < slabs, lambda: stage_a(i, 1 - yl))
-        when(i >= 2, lambda: stage_d(i - 2))
+        when(due, lambda: stage_d(behind))
         return 0
 
-    lax.fori_loop(0, slabs + 2, other_step, 0)
+    lax.fori_loop(0, slabs + LAG[1], other_step, 0)
 
     BR = 64
 
@@ -593,7 +611,7 @@
         compiler_params=pltpu.CompilerParams(
             collective_id=0, has_side_effects=True, vmem_limit_bytes=67_043_328),
         name="gossip",
-    )(mix_numer.reshape(-1), tokens, targets, up_weight, down_weight))
+    )(mix_numer, tokens, targets, up_weight, down_weight))
 
 
 def solution(mesh):

time: 410 us -> 402 us (0.980)
  Pallas kernels: 403 us -> 396 us
    pallas_call x1, Pallas kernels: 397 us -> 390 us  [body(): pl.pallas_call(kernel, out_shape=jax.ShapeDtypeStruct(down_weight.shape,...]
where the time goes in v6:
time: 402 us; the launch traced here: 398 us
  Pallas kernels  396 us (99%)
    pallas_call x1, Pallas kernels, body(): pl.pallas_call(kernel, out_shape=jax.ShapeDtypeStruct(down_weight.shape,...  390 us

profile of v6, /device:TPU:120, one launch (start us, length us, event | category | flops | bytes accessed | tf_op | source)
XLA Modules:
  0.0 397.8 jit_solution(6962078102155922210)
XLA Ops:
  0.0 1.4 copy.6.numer
  1.4 390.4 %gossip.1.src = bf16[1,1792,2048]{2,1,0:T(8,128)(2,1)} custom-call(s32[2,32,3]{2,1,0:T(8,128)} %copy.6.numer, bf16[256,2048]{1,0:T(8,128)(2,1)} %tokens.1, bf16[256,2048]{1,0:T(8,128)(2,1)} %targets.1, bf16[2048,1792]{1,0:T(8,128)(2,1)} %up.1, bf16[1,1792,2048]{2,1,0:T(8,128)(2,1)} %weight.1), custom_call_target="tpu_custom_call" | custom-call | tf_op jit(solution)/shard_map/gossip/pallas_call | solution.py:594
  391.8 6.0 %place.1 = bf16[1,1792,2048]{2,1,0:T(8,128)(2,1)} custom-call(bf16[1,1792,2048]{2,1,0:T(8,128)(2,1)} %gossip.1.src), custom_call_target="tpu_custom_call" | custom-call | tf_op jit(solution)/shard_map/place/pallas_call | solution.py:574

commit v7 on v6

--- a/solution.py
+++ b/solution.py
@@ -16,6 +16,7 @@
 LAG = (2, 4)
 HEAD_IN = 4
 PAIR = 2
+LIM = 67_043_328 - 7_800_000
 RING = 4
 LAGS = (0, 2, 3, 6, 7, 8, 9)
 WRAP_DEPTH = 3
@@ -27,10 +28,10 @@
     return jnp.dot(a, b, preferred_element_type=F32)
 
 
-def kernel(numer, tokens, targets, up, weight, out,
-           s, l1, r1, l2, r2, avg, rsx, piece, yrx, zrx, tok, hid, qrx, rrx, pown, rel, rels, relr,
+def kernel(numer, tokens, targets, up, weight, l2,
+           s, l1, r1, r2, avg, rsx, piece, yrx, zrx, tok, hid, qrx, rrx, pown, rel, rels, relr,
            ls, ts, tr, ps, pr, qs, qr, rs, rr,
-           gs, gr, xs, xr, as_, ar, ys, yr, zs, zr, os, free):
+           gs, gr, xs, xr, as_, ar, ys, yr, zs, zr, free):
     b, sh = lax.axis_index("blk"), lax.axis_index("shard")
     x, yh, z = b // 8, (b // 4) % 2, b % 4
     yl, e = sh // 2, sh % 2
@@ -365,10 +366,6 @@
         q = r2[c, d, :].astype(F32)
         return m[1][0] * a + m[1][1] * p + m[1][2] * q
 
-    def o_copy(i):
-        c, d = item(i)
-        return pltpu.make_async_copy(l2.at[c, d], out.at[0, d, pl.ds(c * width, width)], os.at[i])
-
     def second(i):
         def inside(c, d):
             l2[c, d, :] = (mixed(c, d) - avg[c, d, :].astype(F32)).astype(BF16)
@@ -378,7 +375,6 @@
 
         when(inner, lambda: over(i, inside))
         when(jnp.logical_not(inner), lambda: over(i, outside))
-        o_copy(i).start()
 
     unmix = 4.0 / jnp.where(z == 1, n(1, kl, 2), n(1, kr, 1))
 
@@ -545,40 +541,28 @@
             for k in range(4):
                 a_x(g, k).wait_send()
 
-    for i in range(chunks, 2 * chunks):
-        o_copy(i).wait()
-
-
-def copy_kernel(src, dst, held, isem, osem):
-    parts = held.shape[0]
-    size = src.shape[1] // parts
-
-    def move(i, back):
-        there = pl.ds(i * size, size)
-        if back:
-            return pltpu.make_async_copy(held.at[i], dst.at[0, there], osem.at[i])
-        return pltpu.make_async_copy(src.at[0, there], held.at[i], isem.at[i])
-
-    for i in range(parts):
-        move(i, False).start()
-    for i in range(parts):
-        move(i, False).wait()
-        move(i, True).start()
-    for i in range(parts):
-        move(i, True).wait()
+
+def copy_kernel(src, dst, sem):
+    slabs, _, width = src.shape
+
+    def move(i):
+        return pltpu.make_async_copy(src.at[i], dst.at[0, :, pl.ds(i * width, width)], sem.at[i])
+
+    for i in range(slabs):
+        move(i).start()
+    for i in range(slabs):
+        move(i).wait()
 
 
 def copy_call(a):
-    parts = 14
-    any_ = pl.BlockSpec(memory_space=pl.ANY)
+    slabs, rows, width = a.shape
     return pl.pallas_call(
         copy_kernel,
-        out_shape=jax.ShapeDtypeStruct(a.shape, a.dtype),
-        in_specs=[any_],
-        out_specs=any_,
-        scratch_shapes=[pltpu.VMEM((parts, a.shape[1] // parts, a.shape[2]), a.dtype),
-                        pltpu.SemaphoreType.DMA((parts,)), pltpu.SemaphoreType.DMA((parts,))],
-        compiler_params=pltpu.CompilerParams(vmem_limit_bytes=67_043_328),
+        out_shape=jax.ShapeDtypeStruct((1, rows, slabs * width), a.dtype),
+        in_specs=[pl.BlockSpec(memory_space=pltpu.VMEM)],
+        out_specs=pl.BlockSpec(memory_space=pl.ANY),
+        scratch_shapes=[pltpu.SemaphoreType.DMA((slabs,))],
+        compiler_params=pltpu.CompilerParams(vmem_limit_bytes=8 * 2**20),
         name="place",
     )(a)
 
@@ -593,10 +577,10 @@
     any_ = pl.BlockSpec(memory_space=pl.ANY)
     return copy_call(pl.pallas_call(
         kernel,
-        out_shape=jax.ShapeDtypeStruct(down_weight.shape, BF16),
+        out_shape=pltpu.VMEM((slabs, rows, width), BF16),
         in_specs=[pl.BlockSpec(memory_space=pltpu.SMEM)] + [any_] * 4,
-        out_specs=any_,
-        scratch_shapes=[vm(slabs, rows, width)] * 6 + [
+        out_specs=pl.BlockSpec(memory_space=pltpu.VMEM),
+        scratch_shapes=[vm(slabs, rows, width)] * 5 + [
             vm(3, RING, rows // 4, width), vm(slabs, rows // 4, width),
             vm(slabs, rows // 8, width), vm(slabs, rows // 8, width),
             vm(4 * trow, dim), vm(4 * trow, rows),
@@ -605,11 +589,11 @@
             D((5, slabs)), D((3, 2)), D((3, 2)),
             D((slabs, 2)), D((slabs, 2)), D((slabs, 2)), D((slabs, 2)), D((slabs,)), D((slabs,)),
             D((2, 4 * slabs)), D((2, 4 * slabs)), D((slabs, 3)), D((slabs, 3)), D((slabs, 4)), D((slabs, 4)),
-            D((2, slabs)), D((2, slabs)), D((slabs,)), D((slabs,)), D((4 * slabs,)),
+            D((2, slabs)), D((2, slabs)), D((slabs,)), D((slabs,)),
             pltpu.SemaphoreType.REGULAR((slabs - RING,)),
         ],
         compiler_params=pltpu.CompilerParams(
-            collective_id=0, has_side_effects=True, vmem_limit_bytes=67_043_328),
+            collective_id=0, has_side_effects=True, vmem_limit_bytes=LIM),
         name="gossip",
     )(mix_numer, tokens, targets, up_weight, down_weight))
 

time: 402 us -> 398 us (0.990)
  no operation moved by 1% of the time
where the time goes in v7:
time: 398 us; the launch traced here: 394 us
  Pallas kernels  393 us (99%)
    pallas_call x1, Pallas kernels, body(): pl.pallas_call(kernel, out_shape=pltpu.VMEM((slabs, rows, width), BF16),...  390 us

profile of v7, /device:TPU:120, one launch (start us, length us, event | category | flops | bytes accessed | tf_op | source)
XLA Modules:
  0.0 394.0 jit_solution(748093452197592585)
XLA Ops:
  0.0 1.4 copy.6.numer
  1.4 389.6 %gossip.1.src = bf16[8,1792,256]{2,1,0:T(8,128)(2,1)S(1)} custom-call(s32[2,32,3]{2,1,0:T(8,128)} %copy.6.numer, bf16[256,2048]{1,0:T(8,128)(2,1)} %tokens.1, bf16[256,2048]{1,0:T(8,128)(2,1)} %targets.1, bf16[2048,1792]{1,0:T(8,128)(2,1)} %up.1, bf16[1,1792,2048]{2,1,0:T(8,128)(2,1)} %weight.1), custom_call_target="tpu_custom_call" | custom-call | tf_op jit(solution)/shard_map/gossip/pallas_call | solution.py:578
  391.0 3.1 place.1

commit v8 on v7

--- a/solution.py
+++ b/solution.py
@@ -122,7 +122,7 @@
         t_in(c).start()
 
     def n(r, k, j):
-        return numer[r, k, j].astype(F32)
+        return numer[j, r, k].astype(F32)
 
     kl, kr, kll, krr = (b + 31) % 32, (b + 1) % 32, (b + 30) % 32, (b + 2) % 32
 
@@ -595,7 +595,7 @@
         compiler_params=pltpu.CompilerParams(
             collective_id=0, has_side_effects=True, vmem_limit_bytes=LIM),
         name="gossip",
-    )(mix_numer, tokens, targets, up_weight, down_weight))
+    )(mix_numer.transpose(2, 0, 1), tokens, targets, up_weight, down_weight))
 
 
 def solution(mesh):

time: 398 us -> 396 us (level)
  no operation moved by 1% of the time
where the time goes in v8:
time: 396 us; the launch traced here: 392 us
  Pallas kernels  392 us (99%)
    pallas_call x1, Pallas kernels, body(): pl.pallas_call(kernel, out_shape=pltpu.VMEM((slabs, rows, width), BF16),...  389 us

profile of v8, /device:TPU:120, one launch (start us, length us, event | category | flops | bytes accessed | tf_op | source)
XLA Modules:
  0.0 392.1 jit_solution(647680518790587963)
XLA Ops:
  0.0 389.1 %gossip.1.src = bf16[8,1792,256]{2,1,0:T(8,128)(2,1)S(1)} custom-call(s32[3,2,32]{2,1,0:T(2,128)} %bitcast.1, bf16[256,2048]{1,0:T(8,128)(2,1)} %tokens.1, bf16[256,2048]{1,0:T(8,128)(2,1)} %targets.1, bf16[2048,1792]{1,0:T(8,128)(2,1)} %up.1, bf16[1,1792,2048]{2,1,0:T(8,128)(2,1)} %weight.1), custom_call_target="tpu_custom_call" | custom-call | tf_op jit(solution)/shard_map/gossip/pallas_call | solution.py:578
  389.1 3.1 place.1

commit v9 on v8

--- a/solution.py
+++ b/solution.py
@@ -12,7 +12,7 @@
 NW = 32
 GRAD_ROWS = 896
 HEAD = 4
-RELAY_AT = 3
+RELAY_AT = 1
 LAG = (2, 4)
 HEAD_IN = 4
 PAIR = 2
@@ -320,11 +320,9 @@
         when(jnp.logical_and(i >= 1, i <= slabs), lambda: stage_b(i - 1, 1 - yl),
              lambda: c_q(i - 1, 1 - yl).start())
 
-        @pl.when(jnp.logical_and(i == RELAY_AT, inner))
-        def _():
-            for k in range(slabs - HEAD):
-                relay_out(HEAD + k).wait_recv()
-                relay_on(k).start()
+        for k in range(slabs - HEAD):
+            when(jnp.logical_and(i == RELAY_AT + k, inner),
+                 lambda: relay_out(HEAD + k).wait_recv(), lambda: relay_on(k).start())
 
         when(jnp.logical_and(jnp.logical_and(i >= 1, i <= slabs - HEAD_IN), inner),
              lambda: c_q(i - 1 + HEAD_IN, yl).start())

time: 396 us -> 396 us (level)
  no operation moved by 1% of the time
where the time goes in v9:
time: 396 us; the launch traced here: 392 us
  Pallas kernels  392 us (99%)
    pallas_call x1, Pallas kernels, body(): pl.pallas_call(kernel, out_shape=pltpu.VMEM((slabs, rows, width), BF16),...  389 us

profile of v9, /device:TPU:120, one launch (start us, length us, event | category | flops | bytes accessed | tf_op | source)
XLA Modules:
  0.0 392.2 jit_solution(10548453117541656236)
XLA Ops:
  0.0 389.1 %gossip.1.src = bf16[8,1792,256]{2,1,0:T(8,128)(2,1)S(1)} custom-call(s32[3,2,32]{2,1,0:T(2,128)} %bitcast.1, bf16[256,2048]{1,0:T(8,128)(2,1)} %tokens.1, bf16[256,2048]{1,0:T(8,128)(2,1)} %targets.1, bf16[2048,1792]{1,0:T(8,128)(2,1)} %up.1, bf16[1,1792,2048]{2,1,0:T(8,128)(2,1)} %weight.1), custom_call_target="tpu_custom_call" | custom-call | tf_op jit(solution)/shard_map/gossip/pallas_call | solution.py:576
  389.1 3.1 place.1
